TPU v7x, 128 devices: a whole 4x4x4 slice. The times are simulated.
128 devices in a mesh: dp: 1, node: 2 (over core), ep: 64 (over z, y, x).
Axes of the slice: x: 4, y: 4, z: 4, core: 2. Of those that a mesh axis runs over, the one named last changes fastest.
Arguments:
- tokens: bfloat16 [32768, 2048], P(('dp', 'node', 'ep'))
- expert_ids: int32 [32768, 8], P(('dp', 'node', 'ep'))
- route_w: float32 [32768, 8], P(('dp', 'node', 'ep'))
- node_slot: int32 [32768, 8], P(('dp', 'node', 'ep'))
- exp_slot: int32 [32768, 8], P(('dp', 'node', 'ep'))
- w_gate: bfloat16 [128, 2048, 768], P(('node', 'ep'))
- w_up: bfloat16 [128, 2048, 768], P(('node', 'ep'))
- w_down: bfloat16 [128, 768, 2048], P(('node', 'ep'))
Outputs:
- output: bfloat16 [32768, 2048], P(('dp', 'node', 'ep'))
All inputs are finite; a program needn't handle non-finite values.
Results may differ from a plain program's by a relative error of at most 0.00151.
Values are sent between devices in bfloat16 or wider.
A program may use at most 1 GiB of HBM per device.

v0:
```python
import jax
import jax.numpy as jnp
from jax import lax
from jax.sharding import PartitionSpec as P


def value_a10(tok_dev, top_k, num_experts, n_nodes):
    node_limit = max(1, min(top_k, n_nodes // 2))
    cap_node = min(tok_dev, 8 * ((5 * tok_dev * node_limit + 32 * n_nodes - 1) // (32 * n_nodes)))
    cap_exp = 8 * ((5 * n_nodes * tok_dev * top_k + 32 * num_experts - 1) // (32 * num_experts))
    return cap_node, cap_exp


def fill_rows(dest_pos, num_slots):
    n_src, fan_out = dest_pos.shape
    safe_dest = jnp.where(dest_pos >= 0, dest_pos, num_slots)
    src_idx = jnp.full((num_slots,), n_src, jnp.int32).at[safe_dest.reshape(-1)].set(jnp.repeat(jnp.arange(n_src, dtype=jnp.int32), fan_out), mode='drop')
    return jnp.minimum(src_idx, n_src - 1), src_idx < n_src


def solution(mesh):
    n_nodes = mesh.shape['node']
    n_ep = mesh.shape['ep']
    row_spec = P(('dp', 'node', 'ep'), None)
    exp_spec = P(('node', 'ep'), None, None)

    def local_layer(tokens, expert_ids, route_w, node_slot, exp_slot, w_gate, w_up, w_down):
        tok_dev, d_model = tokens.shape
        top_k = expert_ids.shape[1]
        exp_dev = w_gate.shape[0]
        exp_node = exp_dev * n_ep
        cap_node, cap_exp = value_a10(tok_dev, top_k, exp_node * n_nodes, n_nodes)
        node_rows = n_nodes * cap_node
        exp_rows = exp_node * cap_exp
        dst_node = expert_ids // exp_node
        node_ok = node_slot >= 0
        exp_ok = node_ok & (exp_slot >= 0)
        exp_code = jnp.where(exp_ok, (expert_ids % exp_node) * cap_exp + exp_slot, -1)
        row_pos = jnp.where(node_ok, dst_node * cap_node + node_slot, -1)
        src_tok, filled = fill_rows(row_pos, node_rows)
        send_rows = jnp.where(filled[:, None], tokens[src_tok], 0)
        slot_node = jnp.arange(node_rows, dtype=jnp.int32) // cap_node
        row_match = filled[:, None] & (dst_node[src_tok] == slot_node[:, None]) & exp_ok[src_tok]
        send_code = jnp.where(row_match, exp_code[src_tok], -1)
        send_wt = jnp.where(row_match, route_w[src_tok], 0.0)
        recv_rows = lax.all_to_all(send_rows, 'node', 0, 0, tiled=True)
        recv_code = lax.all_to_all(send_code, 'node', 0, 0, tiled=True)
        recv_wt = lax.all_to_all(send_wt, 'node', 0, 0, tiled=True)
        src_row, filled_exp = fill_rows(recv_code, exp_rows)
        send_exp = jnp.where(filled_exp[:, None], recv_rows[src_row], 0)
        recv_exp = lax.all_to_all(send_exp, 'ep', 0, 0, tiled=True).reshape(n_ep, exp_dev, cap_exp, d_model)
        gate_act = jnp.einsum('gecd,edf->egcf', recv_exp, w_gate, preferred_element_type=jnp.float32)
        up_act = jnp.einsum('gecd,edf->egcf', recv_exp, w_up, preferred_element_type=jnp.float32)
        hidden = (jax.nn.silu(gate_act) * up_act).astype(jnp.bfloat16)
        exp_out = jnp.einsum('egcf,efd->gecd', hidden, w_down, preferred_element_type=jnp.float32).astype(jnp.bfloat16)
        back_exp = lax.all_to_all(exp_out.reshape(exp_rows, d_model), 'ep', 0, 0, tiled=True)
        picked = back_exp[jnp.clip(recv_code, 0, exp_rows - 1)]
        partial = jnp.sum(recv_wt[:, :, None] * picked, axis=1).astype(jnp.bfloat16)
        back_node = lax.all_to_all(partial, 'node', 0, 0, tiled=True)
        same_node = dst_node[:, :, None] == dst_node[:, None, :]
        earlier = jnp.arange(top_k)[None, :] < jnp.arange(top_k)[:, None]
        first_on = jnp.logical_not(jnp.any(same_node & earlier[None], axis=2)) & node_ok
        node_back_rows = back_node[jnp.clip(row_pos, 0, node_rows - 1)]
        return jnp.sum(jnp.where(first_on[:, :, None], node_back_rows.astype(jnp.float32), 0.0), axis=1).astype(jnp.bfloat16)

    return jax.shard_map(local_layer, mesh=mesh, in_specs=(row_spec,) * 5 + (exp_spec,) * 3, out_specs=row_spec, check_vma=False)
```

profile of v0, /device:TPU:57, one launch (start us, length us, event | category | flops | bytes accessed | tf_op | source)
XLA Modules:
  0.0 515.0 jit_solution(4653470710071665261)
XLA Ops:
  1.3 8.0 %scatter_custom_fusion = s32[320]{0:T(512)S(1)} fusion(s32[2048]{0:T(1024)S(1)} %bitcast.46, s32[2048]{0:T(1024)S(1)} %reshape.278, s32[]{:T(128)} %constant.36.clone.1), kind=kCustom, calls=%fused_computation.61 | custom fusion | bytes 1284 | tf_op jit(solution)/shard_map/scatter | solution.py:17
  9.5 1.1 gather_fusion
  10.9 1.2 gather_fusion.1
  13.1 1.1 gather_fusion.2
  14.5 1.1 gather_fusion.3
  16.9 3.9 all-to-all-start.1
  20.8 6.3 %gather_fusion.4 = bf16[320,2048]{1,0:T(8,128)(2,1)} fusion(bf16[256,2048]{1,0:T(8,128)(2,1)} %param.8, s32[1024]{0:T(1024)S(1)} %pad_clamp_fusion.2), kind=kCustom, calls=%fused_computation.4 | custom fusion | bytes 2622720 | tf_op jit(solution)/shard_map/gather | solution.py:41
  27.1 2.5 broadcast_select_fusion.1
  29.7 4.5 all-to-all-start.2
  34.7 9.9 %scatter_custom_fusion.1 = s32[2560]{0:T(1024)S(1)} fusion(s32[2560]{0:T(1024)S(1)} %fusion.6, s32[2560]{0:T(1024)S(1)} %reshape.286, s32[]{:T(128)} %constant.66.clone.1), kind=kCustom, calls=%fused_computation.51 | custom fusion | bytes 10244 | tf_op jit(solution)/shard_map/scatter | solution.py:17
  44.8 21.6 %gather_fusion.5 = bf16[2560,2048]{1,0:T(8,128)(2,1)} fusion(bf16[320,2048]{1,0:T(8,128)(2,1)} %bitcast.7, s32[3072]{0:T(1024)S(1)} %pad_clamp_fusion.1), kind=kCustom, calls=%fused_computation.5 | custom fusion | bytes 20981760 | tf_op jit(solution)/shard_map/gather | solution.py:50
  66.4 5.6 %broadcast_select_fusion = bf16[64,40,2048]{2,1,0:T(8,128)(2,1)S(1)} fusion(bf16[64,40,2048]{2,1,0:T(8,128)(2,1)} %bitcast.38, pred[64,40]{1,0:T(8,128)(4,1)S(1)} %broadcast_in_dim.98), kind=kLoop, calls=%fused_computation.14 | loop fusion | flops 5242880 | bytes 20974080 | tf_op jit(solution)/shard_map/jit(_where)/select_n | solution.py:50
  72.1 146.8 %all_to_all.48 = bf16[64,40,2048]{2,1,0:T(8,128)(2,1)} all-to-all(bf16[64,40,2048]{2,1,0:T(8,128)(2,1)S(1)} %broadcast_select_fusion), channel_id=1, replica_groups=mesh['dp'=1,'node'=2,'ep'=64] {'ep'}, dimensions={0} | all-to-all | bytes 20971520 | tf_op jit(solution)/shard_map/all_to_all | solution.py:51
  218.8 4.8 all-to-all-start
  223.6 12.3 %fusion.3 = f32[64,40,768]{2,1,0:T(8,128)S(1)} fusion(bf16[64,40,2048]{2,1,0:T(8,128)(2,1)} %all_to_all.48, bf16[1,2048,768]{2,1,0:T(8,128)(2,1)} %param.14), kind=kOutput, calls=%fused_computation.18 | convolution fusion | flops 8053063680 | bytes 21495808 | tf_op jit(solution)/shard_map/gecd,edf->egcf/dot_general | solution.py:53
  235.9 11.0 %multiply_convert_fusion = bf16[64,40,768]{2,1,0:T(8,128)(2,1)} fusion(f32[64,40,768]{2,1,0:T(8,128)S(1)} %fusion.3, bf16[64,40,2048]{2,1,0:T(8,128)(2,1)S(1)} %copy-done.2, bf16[1,2048,768]{2,1,0:T(8,128)(2,1)S(1)} %copy-done.4), kind=kOutput, calls=%fused_computation.15 | convolution fusion | flops 8064860160 | bytes 25427968 | tf_op jit(solution)/shard_map/gecd,edf->egcf/dot_general | solution.py:52
  246.9 13.1 %convolution_convert_fusion = bf16[64,40,2048]{2,1,0:T(8,128)(2,1)} fusion(bf16[64,40,768]{2,1,0:T(8,128)(2,1)} %multiply_convert_fusion, bf16[1,768,2048]{2,1,0:T(8,128)(2,1)S(1)} %copy-done), kind=kOutput, calls=%fused_computation.16 | convolution fusion | flops 8058306560 | bytes 17563648 | tf_op jit(solution)/shard_map/egcf,efd->gecd/dot_general | solution.py:55
  260.0 8.5 %all-to-all-start.4 = ((bf16[64,40,2048]{2,1,0:T(8,128)(2,1)}), bf16[64,40,2048]{2,1,0:T(8,128)(2,1)}, u32[]{:S(2)}, u32[]{:S(2)}) async-start(bf16[64,40,2048]{2,1,0:T(8,128)(2,1)} %convolution_convert_fusion), calls=%async_computation.4 | async-start | bytes 20971520 | tf_op jit(solution)/shard_map/all_to_all | solution.py:56
  269.6 168.9 %all-to-all-done.4 = bf16[64,40,2048]{2,1,0:T(8,128)(2,1)} async-done(((bf16[64,40,2048]{2,1,0:T(8,128)(2,1)}), bf16[64,40,2048]{2,1,0:T(8,128)(2,1)}, u32[]{:S(2)}, u32[]{:S(2)}) %all-to-all-start.4) | async-done | bytes 10485792 | tf_op jit(solution)/shard_map/all_to_all | solution.py:56
  438.5 25.5 %gather_fusion.6 = bf16[2560,2048]{1,0:T(8,128)(2,1)} fusion(bf16[2560,2048]{1,0:T(8,128)(2,1)} %bitcast.15, s32[3072]{0:T(1024)S(1)} %pad_clamp_fusion), kind=kCustom, calls=%fused_computation.6 | custom fusion | bytes 20981760 | tf_op jit(solution)/shard_map/gather | solution.py:57
  464.0 9.9 %fusion = bf16[320,2048]{1,0:T(8,128)(2,1)S(1)} fusion(bf16[2560,2048]{1,0:T(8,128)(2,1)} %gather_fusion.6, f32[320,8]{1,0:T(8,128)S(1)} %bitcast.44), kind=kLoop, calls=%fused_computation.11 | loop fusion | flops 15073280 | bytes 11806720 | tf_op jit(solution)/shard_map/reduce_sum | solution.py:58
  473.9 9.7 %all_to_all.49 = bf16[2,160,2048]{2,1,0:T(8,128)(2,1)} all-to-all(bf16[2,160,2048]{2,1,0:T(8,128)(2,1)S(1)} %bitcast.40), channel_id=1, replica_groups=mesh['dp'=1,'node'=2,'ep'=64] {'node'}, dimensions={0} | all-to-all | bytes 2621440 | tf_op jit(solution)/shard_map/all_to_all | solution.py:59
  483.6 18.0 %gather_fusion.7 = bf16[2048,2048]{1,0:T(8,128)(2,1)} fusion(bf16[320,2048]{1,0:T(8,128)(2,1)} %bitcast.37, s32[2048]{0:T(1024)S(1)} %broadcast_clamp_fusion.1), kind=kCustom, calls=%fused_computation.7 | custom fusion | bytes 16785408 | tf_op jit(solution)/shard_map/gather | solution.py:63
  501.6 13.0 %fusion.1 = bf16[256,2048]{1,0:T(8,128)(2,1)} fusion(bf16[2048,2048]{1,0:T(8,128)(2,1)} %gather_fusion.7, pred[256,8]{1,0:T(8,128)(4,1)S(1)} %copy.105), kind=kLoop, calls=%fused_computation.13 | loop fusion | flops 12058624 | bytes 9439232 | tf_op jit(solution)/shard_map/reduce_sum | solution.py:64
  (58 shorter events, 5.8 us)
Async XLA Ops:
  0.0 246.9 %copy-start = (bf16[1,768,2048]{2,1,0:T(8,128)(2,1)S(1)}, bf16[1,768,2048]{2,1,0:T(8,128)(2,1)}, u32[]{:S(2)}) copy-start(bf16[1,768,2048]{2,1,0:T(8,128)(2,1)} %param.15) | copy-start | bytes 9437188
  16.9 12.8 %all-to-all-start.1 = ((s32[2,160,8]{1,2,0:T(8,128)}), s32[2,160,8]{1,2,0:T(8,128)S(1)}, u32[]{:S(2)}, u32[]{:S(2)}) async-start(s32[2,160,8]{1,2,0:T(8,128)} %broadcast_select_fusion.2), calls=%async_computation.1 | async-start | bytes 32768 | tf_op jit(solution)/shard_map/all_to_all | solution.py:47
  29.7 15.1 %all-to-all-start.2 = ((bf16[2,160,2048]{2,1,0:T(8,128)(2,1)}), bf16[2,160,2048]{2,1,0:T(8,128)(2,1)}, u32[]{:S(2)}, u32[]{:S(2)}) async-start(bf16[2,160,2048]{2,1,0:T(8,128)(2,1)} %broadcast_select_fusion.1), calls=%async_computation.2 | async-start | bytes 2621440 | tf_op jit(solution)/shard_map/all_to_all | solution.py:46
  218.8 41.1 %all-to-all-start = ((f32[2,160,8]{1,2,0:T(8,128)}), f32[2,160,8]{1,2,0:T(8,128)S(1)}, u32[]{:S(2)}, u32[]{:S(2)}) async-start(f32[2,160,8]{1,2,0:T(8,128)} %get-tuple-element.5), calls=%async_computation | async-start | bytes 32768 | tf_op jit(solution)/shard_map/all_to_all | solution.py:48
  223.6 12.3 %copy-start.2 = (bf16[64,40,2048]{2,1,0:T(8,128)(2,1)S(1)}, bf16[64,40,2048]{2,1,0:T(8,128)(2,1)}, u32[]{:S(2)}) copy-start(bf16[64,40,2048]{2,1,0:T(8,128)(2,1)} %all_to_all.48) | copy-start | bytes 31457284
  223.6 12.3 %copy-start.4 = (bf16[1,2048,768]{2,1,0:T(8,128)(2,1)S(1)}, bf16[1,2048,768]{2,1,0:T(8,128)(2,1)}, u32[]{:S(2)}) copy-start(bf16[1,2048,768]{2,1,0:T(8,128)(2,1)} %param.13) | copy-start | bytes 9437188
  260.0 9.2 %copy-start.3 = (s32[256,8]{0,1:T(8,128)S(1)}, s32[256,8]{0,1:T(8,128)}, u32[]{:S(2)}) copy-start(s32[256,8]{0,1:T(8,128)} %param.11) | copy-start | bytes 24580
  260.0 178.5 %all-to-all-start.4 = ((bf16[64,40,2048]{2,1,0:T(8,128)(2,1)}), bf16[64,40,2048]{2,1,0:T(8,128)(2,1)}, u32[]{:S(2)}, u32[]{:S(2)}) async-start(bf16[64,40,2048]{2,1,0:T(8,128)(2,1)} %convolution_convert_fusion), calls=%async_computation.4 | async-start | bytes 20971520 | tf_op jit(solution)/shard_map/all_to_all | solution.py:56
  483.6 31.0 %copy-start.1 = (bf16[1,768,2048]{2,1,0:T(8,128)(2,1)S(1)}, bf16[1,768,2048]{2,1,0:T(8,128)(2,1)}, u32[]{:S(2)}) copy-start(bf16[1,768,2048]{2,1,0:T(8,128)(2,1)} %param.15) | copy-start | bytes 9437188
where the time goes:
time: 520 us; the launch traced here: 515 us
  waiting for transfers between devices  169 us (32%)
  blocking collectives  156 us (30%)
  local copies, waits for them, and re-layouts  97.3 us (19%)
  matrix products  36.3 us (7%)
  other arithmetic  33.5 us (6%)
  starting transfers between devices  21.7 us (4%)
    all_to_all x1, waiting for transfers between devices, local_layer(): lax.all_to_all(exp_out.reshape(exp_rows, d_model), 'ep', 0, 0, tiled=True)  169 us
    all_to_all x1, blocking collectives, local_layer(): lax.all_to_all(send_exp, 'ep', 0, 0, tiled=True)  147 us
    gather x1, local copies, waits for them, and re-layouts, local_layer(): picked = back_exp[jnp.clip(recv_code, 0, exp_rows - 1)]  25.5 us
    gather x1, local copies, waits for them, and re-layouts, local_layer(): send_exp = jnp.where(filled_exp[:, None], recv_rows[src_row], 0)  21.6 us
    gather x1, local copies, waits for them, and re-layouts, local_layer(): node_back_rows = back_node[jnp.clip(row_pos, 0, node_rows - 1)]  18 us
    scatter x2, local copies, waits for them, and re-layouts, fill_rows(): jnp.full((num_slots,), n_src, jnp.int32).at[safe_dest.reshape(-1)]  18 us
    dot_general x1, matrix products, local_layer(): jnp.einsum('egcf,efd->gecd', hidden, w_down, preferred_element_type=jnp.f...  13.1 us
    reduce_sum x1, other arithmetic, local_layer(): jnp.sum(jnp.where(first_on[:, :, None], node_back_rows.astype(jnp.float32...  13 us
  transfers between devices with their start and end apart: 4, of which 1 were waited for; matrix products, arithmetic and copies ran while one was open for 11% of the time, Pallas kernels for 0%

commit v1 on v0

v1 whole, which is shorter than its diff:
```python
import functools

import jax
import jax.numpy as jnp
from jax import lax
from jax.experimental import pallas as pl
from jax.experimental.pallas import tpu as pltpu
from jax.sharding import PartitionSpec as P

MESH = pl.DeviceIdType.MESH
SIDE = 4
SHIFTS = (1, 3, 2)
ROUTES = ((2, 1, 0), (1, 0, 2), (0, 2, 1))
BLK = 8


def part_columns(d_model):
    tiles = d_model // 128
    base, extra = tiles // 3, tiles % 3
    cols, at = [], 0
    for k in range(3):
        width = (base + (1 if k >= 3 - extra else 0)) * 128
        cols.append((at, width))
        at += width
    return cols


def moe_kernel(dims, tok_hbm, meta_hbm, metat_hbm, wg_hbm, wu_hbm, wd_hbm, out_ref, mid_d, mid_r,
               tok, meta, metat, wg, wu, wd, send0, hop, work, back, hid, acc, p_send, p_recv,
               in_sem, w_sem, own_sem, send_sem, recv_sem, pair_send, pair_recv):
    n_chunks, n_ep, node_stride, slot_stride, top_k = dims
    tok_dev, d_model = tok_hbm.shape
    d_ff = wg_hbm.shape[1]
    rows = n_ep * BLK
    node = lax.axis_index("node")
    ep = lax.axis_index("ep")
    pos = (ep // (SIDE * SIDE), (ep // SIDE) % SIDE, ep % SIDE)
    cols = part_columns(d_model)
    other = 1 - node

    def peer(dim, shift):
        at = [pos[0], pos[1], pos[2]]
        at[dim] = (pos[dim] + shift) % SIDE
        return (at[0] * SIDE + at[1]) * SIDE + at[2]

    def plane(ref, chunk, dim, index, part):
        c0, width = cols[part]
        idx = [chunk, slice(None), slice(None), slice(None), slice(None), pl.ds(c0, width)]
        idx[1 + dim] = index
        return ref.at[tuple(idx)]

    weights = [pltpu.make_async_copy(s, d, w_sem.at[i]) for i, (s, d) in enumerate(((wg_hbm, wg), (wu_hbm, wu), (wd_hbm, wd)))]
    inputs = ((tok_hbm, tok), (meta_hbm, meta), (metat_hbm, metat))
    local_in = [pltpu.make_async_copy(s, d.at[node], in_sem.at[i]) for i, (s, d) in enumerate(inputs)]
    pair_in = [pltpu.make_async_remote_copy(src_ref=s, dst_ref=d.at[node], send_sem=pair_send.at[i], recv_sem=pair_recv.at[i],
                                            device_id={"node": other}, device_id_type=MESH) for i, (s, d) in enumerate(inputs)]
    for c in local_in:
        c.start()
    barrier = pltpu.get_barrier_semaphore()
    pl.semaphore_signal(barrier, inc=1, device_id={"node": other}, device_id_type=MESH)
    for dim in range(3):
        for shift in SHIFTS:
            pl.semaphore_signal(barrier, inc=1, device_id={"ep": peer(dim, shift)}, device_id_type=MESH)
    pl.semaphore_wait(barrier, 1 + 3 * len(SHIFTS))
    for c in pair_in:
        c.start()
    for c in weights:
        c.start()
    acc[...] = jnp.zeros_like(acc)
    for c in local_in:
        c.wait()
    for c in pair_in:
        c.wait()

    stages = ((send0, 2, hop, 0), (hop, n_chunks, mid_d, 1), (mid_d, n_chunks, work, 2),
              (work, n_chunks, hop, 2), (hop, n_chunks, mid_r, 1), (mid_r, n_chunks, back, 0))

    def copies(stage, chunk):
        src, src_slots, dst, leg = stages[stage]
        src_chunk = chunk % src_slots if src_slots == 2 else chunk
        remote, local = [], []
        for part in range(3):
            dim = ROUTES[part][leg]
            for v, shift in enumerate(SHIFTS):
                remote.append(pltpu.make_async_remote_copy(
                    src_ref=plane(src, src_chunk, dim, (pos[dim] + shift) % SIDE, part),
                    dst_ref=plane(dst, chunk, dim, pos[dim], part),
                    send_sem=send_sem.at[stage, chunk % 2, part, v],
                    recv_sem=recv_sem.at[stage, chunk, part, v],
                    device_id={"ep": peer(dim, shift)}, device_id_type=MESH))
            local.append(pltpu.make_async_copy(
                plane(src, src_chunk, dim, pos[dim], part), plane(dst, chunk, dim, pos[dim], part),
                own_sem.at[stage, chunk % 2, part]))
        return remote, local

    def launch(stage, chunk):
        remote, local = copies(stage, chunk)
        for c in remote:
            c.start()
        for c in local:
            c.start()

    def finish(stage, chunk):
        remote, local = copies(stage, chunk)
        for c in remote:
            c.wait()
        for c in local:
            c.wait()

    base = (node * node_stride).astype(jnp.float32)

    def gather(chunk):
        row = lax.broadcasted_iota(jnp.int32, (rows, tok_dev), 0)
        want = ((row // BLK) * slot_stride + row % BLK + chunk * BLK).astype(jnp.float32) + base
        picks = []
        for n in range(2):
            hit = jnp.zeros((rows, tok_dev), jnp.float32)
            for j in range(top_k):
                hit = jnp.where(metat[n, j:j + 1, :] == want, 1.0, hit)
            picks.append(hit.astype(jnp.bfloat16))
        width = 512
        for n in range(d_model // width):
            block = (jnp.dot(picks[0], tok[0, :, n * width:(n + 1) * width], preferred_element_type=jnp.float32)
                     + jnp.dot(picks[1], tok[1, :, n * width:(n + 1) * width], preferred_element_type=jnp.float32))
            send0[chunk % 2, :, :, :, :, n * width:(n + 1) * width] = block.reshape(SIDE, SIDE, SIDE, BLK, width).astype(jnp.bfloat16)

    def ffn(chunk):
        width = 256

        def up(n, carry):
            at = pl.ds(pl.multiple_of(n * width, width), width)
            x = work[chunk].reshape(rows, d_model)
            g = jnp.dot(x, wg[:, at], preferred_element_type=jnp.float32)
            u = jnp.dot(x, wu[:, at], preferred_element_type=jnp.float32)
            hid[:, at] = (jax.nn.silu(g) * u).astype(jnp.bfloat16)
            return carry

        lax.fori_loop(0, d_ff // width, up, 0)

        def down(n, carry):
            at = pl.ds(pl.multiple_of(n * width, width), width)
            y = jnp.dot(hid[...], wd[:, at], preferred_element_type=jnp.float32)
            work[chunk, :, :, :, :, at] = y.reshape(SIDE, SIDE, SIDE, BLK, width).astype(jnp.bfloat16)
            return carry

        lax.fori_loop(0, d_model // width, down, 0)

    def combine(chunk):
        lane = lax.broadcasted_iota(jnp.int32, (tok_dev, rows), 1)
        want = ((lane // BLK) * slot_stride + lane % BLK + chunk * BLK).astype(jnp.float32) + base
        width = 512
        for n in range(2):
            mix = jnp.zeros((tok_dev, rows), jnp.float32)
            for j in range(top_k):
                mix = jnp.where(meta[n, :, j:j + 1] == want, meta[n, :, top_k + j:top_k + j + 1], mix)
            hi = mix.astype(jnp.bfloat16)
            rest = mix - hi.astype(jnp.float32)
            mid = rest.astype(jnp.bfloat16)
            lo = (rest - mid.astype(jnp.float32)).astype(jnp.bfloat16)
            for q in range(d_model // width):
                at = slice(q * width, (q + 1) * width)
                y = back[chunk, :, :, :, :, at].reshape(rows, width)
                add = jnp.dot(lo, y, preferred_element_type=jnp.float32)
                add = add + jnp.dot(mid, y, preferred_element_type=jnp.float32)
                add = add + jnp.dot(hi, y, preferred_element_type=jnp.float32)
                acc[n, :, at] += add

    def step(t, carry):
        @pl.when(t < n_chunks)
        def _():
            gather(t)
            launch(0, t)

        for stage in range(1, 7):
            chunk = t - stage

            @pl.when((chunk >= 0) & (chunk < n_chunks))
            def _():
                finish(stage - 1, chunk)
                if stage == 3:
                    @pl.when(chunk == 0)
                    def _():
                        for c in weights:
                            c.wait()
                    ffn(chunk)
                if stage < 6:
                    launch(stage, chunk)
                else:
                    combine(chunk)
        return carry

    lax.fori_loop(0, n_chunks + 6, step, 0)

    p_send[...] = acc[other].astype(jnp.bfloat16)
    share = pltpu.make_async_remote_copy(src_ref=p_send, dst_ref=p_recv, send_sem=pair_send.at[3], recv_sem=pair_recv.at[3],
                                         device_id={"node": other}, device_id_type=MESH)
    share.start()
    mine = acc[node].astype(jnp.bfloat16).astype(jnp.float32)
    share.wait()
    out_ref[...] = (mine + p_recv[...].astype(jnp.float32)).astype(jnp.bfloat16)


def solution(mesh):
    n_nodes = mesh.shape['node']
    n_ep = mesh.shape['ep']
    row_spec = P(('dp', 'node', 'ep'), None)
    exp_spec = P(('node', 'ep'), None, None)

    def local_layer(tokens, expert_ids, route_w, node_slot, exp_slot, w_gate, w_up, w_down):
        tok_dev, d_model = tokens.shape
        top_k = expert_ids.shape[1]
        d_ff = w_gate.shape[2]
        n_exp = w_gate.shape[0] * n_ep * n_nodes
        cap_exp = 8 * ((5 * n_nodes * tok_dev * top_k + 32 * n_exp - 1) // (32 * n_exp))
        n_chunks = cap_exp // BLK
        slot_stride = 64
        node_stride = n_ep * slot_stride
        rows = n_ep * BLK

        kept = (node_slot >= 0) & (exp_slot >= 0)
        code = jnp.where(kept, expert_ids * slot_stride + exp_slot, -1).astype(jnp.float32)
        weight = jnp.where(kept, route_w, 0.0)
        meta = jnp.pad(jnp.concatenate([code, weight], axis=1), ((0, 0), (0, 128 - 2 * top_k)))
        metat = code.T

        cube = (SIDE, SIDE, SIDE, BLK, d_model)
        bf16, f32 = jnp.bfloat16, jnp.float32
        any_spec = pl.BlockSpec(memory_space=pl.ANY)
        out, _, _ = pl.pallas_call(
            functools.partial(moe_kernel, (n_chunks, n_ep, node_stride, slot_stride, top_k)),
            name="moe_layer",
            out_shape=(jax.ShapeDtypeStruct((tok_dev, d_model), bf16),
                       jax.ShapeDtypeStruct((n_chunks,) + cube, bf16),
                       jax.ShapeDtypeStruct((n_chunks,) + cube, bf16)),
            in_specs=[any_spec] * 6,
            out_specs=(pl.BlockSpec(memory_space=pltpu.VMEM), any_spec, any_spec),
            scratch_shapes=[
                pltpu.VMEM((2, tok_dev, d_model), bf16),
                pltpu.VMEM((2, tok_dev, 128), f32),
                pltpu.VMEM((2, top_k, tok_dev), f32),
                pltpu.VMEM((d_model, d_ff), bf16),
                pltpu.VMEM((d_model, d_ff), bf16),
                pltpu.VMEM((d_ff, d_model), bf16),
                pltpu.VMEM((2,) + cube, bf16),
                pltpu.VMEM((n_chunks,) + cube, bf16),
                pltpu.VMEM((n_chunks,) + cube, bf16),
                pltpu.VMEM((n_chunks,) + cube, bf16),
                pltpu.VMEM((rows, d_ff), bf16),
                pltpu.VMEM((2, tok_dev, d_model), f32),
                pltpu.VMEM((tok_dev, d_model), bf16),
                pltpu.VMEM((tok_dev, d_model), bf16),
                pltpu.SemaphoreType.DMA((3,)),
                pltpu.SemaphoreType.DMA((3,)),
                pltpu.SemaphoreType.DMA((6, 2, 3)),
                pltpu.SemaphoreType.DMA((6, 2, 3, 3)),
                pltpu.SemaphoreType.DMA((6, n_chunks, 3, 3)),
                pltpu.SemaphoreType.DMA((4,)),
                pltpu.SemaphoreType.DMA((4,)),
            ],
            compiler_params=pltpu.CompilerParams(collective_id=0, has_side_effects=True, vmem_limit_bytes=63 * 2**20),
        )(tokens, meta, metat, w_gate[0], w_up[0], w_down[0])
        return out

    return jax.shard_map(local_layer, mesh=mesh, in_specs=(row_spec,) * 5 + (exp_spec,) * 3, out_specs=row_spec, check_vma=False)
```

time: 520 us -> 256 us (0.49)
  the two profiles are of different devices: /device:TPU:57 before, /device:TPU:1 now
where the time goes in v1:
time: 256 us
  Pallas kernels  251 us (98%)
  local copies, waits for them, and re-layouts  3.08 us (1%)
    pallas_call x1, Pallas kernels, local_layer(): pl.pallas_call(functools.partial(moe_kernel, (n_chunks, n_ep, node_stride...  251 us

profile of v1, /device:TPU:1, one launch (start us, length us, event | category | flops | bytes accessed | tf_op | source)
XLA Modules:
  0.0 255.6 jit_solution(8429673228860426429)
XLA Ops:
  0.0 0.7 select_convert_fusion
  0.7 0.0 copy-start
  0.7 0.7 broadcast_select_fusion
  1.4 0.1 copy.10
  1.6 0.7 pad.4.clone.meta_hbm
  2.2 0.0 copy-done
  2.2 251.1 %moe_layer.1 = (bf16[256,2048]{1,0:T(8,128)(2,1)}, bf16[5,4,4,4,8,2048]{5,4,3,2,1,0:T(8,128)(2,1)}, bf16[5,4,4,4,8,2048]{5,4,3,2,1,0:T(8,128)(2,1)}) custom-call(bf16[256,2048]{1,0:T(8,128)(2,1)} %tok_hbm.1, f32[256,128]{1,0:T(8,128)} %pad.4.clone.meta_hbm, f32[8,256]{1,0:T(8,128)} %bitcast.7, bf16[2048,768]{1,0:T(8,128)(2,1)} %bitcast.4, ...), custom_call_target="tpu_custom_call" | custom-call | tf_op jit(solution)/shard_map/moe_layer/pallas_call | solution.py:229
  253.3 2.3 copy.12
  (1 shorter events, 0.0 us)
Async XLA Ops:
  0.7 1.5 copy-start

commit v2 on v1

v2 whole, which is shorter than its diff:
```python
import functools

import jax
import jax.numpy as jnp
from jax import lax
from jax.experimental import pallas as pl
from jax.experimental.pallas import tpu as pltpu
from jax.sharding import PartitionSpec as P

MESH = pl.DeviceIdType.MESH
SIDE = 4
SHIFTS = (1, 3, 2)
ROUTES = ((2, 1, 0), (1, 0, 2), (0, 2, 1))
STRIDE = (16, 4, 1)
BLK = 8
SLOTS = 64
NT = (((1,), (1,)), ((), ()))
TN = (((0,), (0,)), ((), ()))


def part_columns(d_model):
    tiles = d_model // 128
    base, extra = tiles // 3, tiles % 3
    cols, at = [], 0
    for k in range(3):
        width = (base + (1 if k >= 3 - extra else 0)) * 128
        cols.append((at, width))
        at += width
    return cols


def moe_kernel(n_chunks, ids_hbm, rw_hbm, ns_hbm, es_hbm, tok_hbm, wg_hbm, wu_hbm, wd_hbm, out_ref, mid_d, mid_r,
               ids, rw, ns, es, tok, pick, rg0, rg1, rg2, own_codes, codes, c_send, feat, f_send, r_send, p_recv,
               wg, wu, wd, send1, hop, work, back, hid, acc,
               in_sem, w_sem, own_sem, send_sem, recv_sem, pair_send, pair_recv, a_send, a_recv, b_send, b_recv, c_ssem, c_rsem):
    f32, bf16 = jnp.float32, jnp.bfloat16
    tok_dev, d_model = tok_hbm.shape
    d_ff = wg_hbm.shape[1]
    top_k = ids_hbm.shape[0]
    n_ep = SIDE ** 3
    rows = n_ep * BLK
    cap = feat.shape[1]
    half = cap // 2
    node = lax.axis_index("node")
    other = 1 - node
    ep = lax.axis_index("ep")
    pos = (ep // (SIDE * SIDE), (ep // SIDE) % SIDE, ep % SIDE)
    cols = part_columns(d_model)
    rings = (rg0, rg1, rg2)

    def peer(dim, shift):
        at = [pos[0], pos[1], pos[2]]
        at[dim] = (pos[dim] + shift) % SIDE
        return (at[0] * SIDE + at[1]) * SIDE + at[2]

    def to_ep(src, dst, ssem, rsem, dim, shift):
        return pltpu.make_async_remote_copy(src_ref=src, dst_ref=dst, send_sem=ssem, recv_sem=rsem,
                                            device_id={"ep": peer(dim, shift)}, device_id_type=MESH)

    def to_pair(src, dst, i):
        return pltpu.make_async_remote_copy(src_ref=src, dst_ref=dst, send_sem=pair_send.at[i], recv_sem=pair_recv.at[i],
                                            device_id={"node": other}, device_id_type=MESH)

    inputs = [pltpu.make_async_copy(s, d, in_sem.at[i]) for i, (s, d) in enumerate(
        ((ids_hbm, ids), (rw_hbm, rw), (ns_hbm, ns), (es_hbm, es), (tok_hbm, tok)))]
    weights = [pltpu.make_async_copy(s, d, w_sem.at[i]) for i, (s, d) in enumerate(((wg_hbm, wg), (wu_hbm, wu), (wd_hbm, wd)))]
    for c in inputs:
        c.start()
    barrier = pltpu.get_barrier_semaphore()
    pl.semaphore_signal(barrier, inc=1, device_id={"node": other}, device_id_type=MESH)
    for dim in range(3):
        for shift in SHIFTS:
            pl.semaphore_signal(barrier, inc=1, device_id={"ep": peer(dim, shift)}, device_id_type=MESH)
    for c in inputs:
        c.wait()

    def route(m):
        on = (ids[...] >= m * n_ep) & (ids[...] < (m + 1) * n_ep)
        slot = jnp.max(jnp.where(on, ns[...], -1), axis=0, keepdims=True)
        kept = on & (ns[...] >= 0) & (es[...] >= 0)
        a = jnp.where(kept, (ids[...] - m * n_ep) * SLOTS, 0).astype(f32)
        b = jnp.where(kept, es[...] + 1, 0).astype(f32)
        w = jnp.where(kept, rw[...], 0.0)
        w1 = w.astype(bf16).astype(f32)
        w2 = (w - w1).astype(bf16).astype(f32)
        w3 = w - w1 - w2
        fill = jnp.zeros((128 - 2 * top_k, tok_dev), f32)
        parts = [jnp.concatenate([p, q, fill], axis=0).astype(bf16) for p, q in ((a, w1), (b, w2), (jnp.zeros_like(a), w3))]
        hot = jnp.where(lax.broadcasted_iota(jnp.int32, (tok_dev, tok_dev), 0) == slot, 1.0, 0.0).astype(bf16)
        pick[m] = hot[:cap]
        code = sum(lax.dot_general(p, hot, NT, preferred_element_type=f32) for p in parts[:2])[:top_k]
        by_row = sum(lax.dot_general(hot[:cap], p, NT, preferred_element_type=f32) for p in parts[::-1])
        return code, by_row

    own_code, own_feat = route(node)
    for part in range(3):
        c0, width = cols[part]
        rings[part][pos[ROUTES[part][0]], node] = jnp.dot(
            pick[node], tok[:, c0:c0 + width], preferred_element_type=f32).astype(bf16)
    pl.semaphore_wait(barrier, 1 + 3 * len(SHIFTS))

    def ring_copies(part, n):
        dim, ring = ROUTES[part][0], rings[part]
        i = pos[dim]
        first = [to_ep(ring.at[i, n], ring.at[i, n], a_send.at[part, n, v], a_recv.at[part, n, v], dim, (1, 3)[v]) for v in range(2)]
        onward = []
        for v in range(2):
            k = (i + (3, 1)[v]) % SIDE
            span = pl.ds(v * half, half)
            onward.append(to_ep(ring.at[k, n, span], ring.at[k, n, span], b_send.at[part, n, v], b_recv.at[part, n, v], dim, (1, 3)[v]))
        return first, onward

    for part in range(3):
        for c in ring_copies(part, node)[0]:
            c.start()
    own_codes[node] = own_code
    feat[node] = own_feat
    far_code, far_feat = route(other)
    r_send[...] = jnp.dot(pick[other], tok[...], preferred_element_type=f32).astype(bf16)
    c_send[...] = far_code
    f_send[...] = far_feat
    pair = [to_pair(r_send.at[:, pl.ds(*cols[part])], rings[part].at[pos[ROUTES[part][0]], node], part) for part in range(3)]
    pair.append(to_pair(c_send, own_codes.at[node], 3))
    pair.append(to_pair(f_send, feat.at[node], 4))
    for c in pair:
        c.start()
    for c in weights:
        c.start()
    acc[...] = jnp.zeros_like(acc)
    for c in pair:
        c.wait()
    for part in range(3):
        for c in ring_copies(part, other)[0]:
            c.start()
    code_copies = [to_ep(own_codes, codes.at[dim, pos[dim]], c_ssem.at[dim, v], c_rsem.at[dim, v], dim, shift)
                   for dim in range(3) for v, shift in enumerate(SHIFTS)]
    for c in code_copies:
        c.start()
    for dim in range(3):
        codes[dim, pos[dim]] = own_codes[...]
    for n in (node, other):
        for part in range(3):
            first, onward = ring_copies(part, n)
            for v in range(2):
                first[v].wait()
                onward[v].start()
    for c in code_copies:
        c.wait()

    stages = ((send1, mid_d, 1), (mid_d, work, 2), (work, hop, 2), (hop, mid_r, 1), (mid_r, back, 0))

    def plane(ref, chunk, dim, index, part):
        c0, width = cols[part]
        idx = [chunk, slice(None), slice(None), slice(None), slice(None), pl.ds(c0, width)]
        idx[1 + dim] = index
        return ref.at[tuple(idx)]

    def copies(stage, chunk):
        src, dst, leg = stages[stage]
        src_chunk = chunk % 2 if stage == 0 else chunk
        remote, local = [], []
        for part in range(3):
            dim = ROUTES[part][leg]
            for v, shift in enumerate(SHIFTS):
                remote.append(to_ep(plane(src, src_chunk, dim, (pos[dim] + shift) % SIDE, part),
                                    plane(dst, chunk, dim, pos[dim], part),
                                    send_sem.at[stage, chunk % 2, part, v], recv_sem.at[stage, chunk, part, v], dim, shift))
            local.append(pltpu.make_async_copy(
                plane(src, src_chunk, dim, pos[dim], part), plane(dst, chunk, dim, pos[dim], part),
                own_sem.at[stage, chunk % 2, part]))
        return remote, local

    def launch(stage, chunk):
        remote, local = copies(stage, chunk)
        for c in remote:
            c.start()
        for c in local:
            c.start()

    def finish(stage, chunk):
        remote, local = copies(stage, chunk)
        for c in remote:
            c.wait()
        for c in local:
            c.wait()

    def gather(chunk):
        for v in (0, 3, 1, 2):
            if v == 2:
                @pl.when(chunk == 0)
                def _():
                    for n in (node, other):
                        for part in range(3):
                            for c in ring_copies(part, n)[1]:
                                c.wait()
            for part in range(3):
                dim = ROUTES[part][0]
                k = (pos[dim] + v) % SIDE
                c0, width = cols[part]
                o0, o1 = [d for d in range(3) if d != dim]
                r = lax.broadcasted_iota(jnp.int32, (SIDE * SIDE * BLK, cap), 0)
                expert = pos[dim] * STRIDE[dim] + (r >> 5) * STRIDE[o0] + ((r >> 3) & 3) * STRIDE[o1]
                want = (expert * SLOTS + (r & 7) + chunk * BLK + 1).astype(f32)
                block = None
                for n in range(2):
                    hit = jnp.zeros(want.shape, f32)
                    for j in range(top_k):
                        hit = jnp.where(codes[dim, k, n, j:j + 1, :cap] == want, 1.0, hit)
                    got = jnp.dot(hit.astype(bf16), rings[part][k, n], preferred_element_type=f32)
                    block = got if block is None else block + got
                idx = [chunk % 2, slice(None), slice(None), slice(None), slice(None), slice(c0, c0 + width)]
                idx[1 + dim] = k
                send1[tuple(idx)] = block.reshape(SIDE, SIDE, BLK, width).astype(bf16)

    def ffn(chunk):
        width = 256

        def up(n, carry):
            at = pl.ds(pl.multiple_of(n * width, width), width)
            x = work[chunk].reshape(rows, d_model)
            g = jnp.dot(x, wg[:, at], preferred_element_type=f32)
            u = jnp.dot(x, wu[:, at], preferred_element_type=f32)
            hid[:, at] = (jax.nn.silu(g) * u).astype(bf16)
            return carry

        lax.fori_loop(0, d_ff // width, up, 0)

        def down(n, carry):
            at = pl.ds(pl.multiple_of(n * width, width), width)
            y = jnp.dot(hid[...], wd[:, at], preferred_element_type=f32)
            work[chunk, :, :, :, :, at] = y.reshape(SIDE, SIDE, SIDE, BLK, width).astype(bf16)
            return carry

        lax.fori_loop(0, d_model // width, down, 0)

    def combine(chunk):
        lane = lax.broadcasted_iota(jnp.int32, (cap, rows), 1)
        want = ((lane >> 3) * SLOTS + (lane & 7) + chunk * BLK + 1).astype(f32)
        width = 512
        for n in range(2):
            mix = jnp.zeros((cap, rows), f32)
            for j in range(top_k):
                mix = jnp.where(feat[n, :, j:j + 1] == want, feat[n, :, top_k + j:top_k + j + 1], mix)
            hi = mix.astype(bf16)
            rest = mix - hi.astype(f32)
            mid = rest.astype(bf16)
            lo = (rest - mid.astype(f32)).astype(bf16)
            for q in range(d_model // width):
                at = slice(q * width, (q + 1) * width)
                y = back[chunk, :, :, :, :, at].reshape(rows, width)
                add = jnp.dot(lo, y, preferred_element_type=f32)
                add = add + jnp.dot(mid, y, preferred_element_type=f32)
                add = add + jnp.dot(hi, y, preferred_element_type=f32)
                acc[n, :, at] += add

    def step(t, carry):
        @pl.when(t < n_chunks)
        def _():
            gather(t)
            launch(0, t)

        for stage in range(1, 6):
            chunk = t - stage

            @pl.when((chunk >= 0) & (chunk < n_chunks))
            def _():
                finish(stage - 1, chunk)
                if stage == 2:
                    @pl.when(chunk == 0)
                    def _():
                        for c in weights:
                            c.wait()
                    ffn(chunk)
                if stage < 5:
                    launch(stage, chunk)
                else:
                    combine(chunk)
        return carry

    lax.fori_loop(0, n_chunks + 5, step, 0)

    r_send[...] = acc[other].astype(bf16)
    share = to_pair(r_send, p_recv, 5)
    share.start()
    mine = lax.dot_general(pick[node], acc[node].astype(bf16), TN, preferred_element_type=f32)
    share.wait()
    theirs = lax.dot_general(pick[other], p_recv[...], TN, preferred_element_type=f32)
    out_ref[...] = (mine + theirs).astype(bf16)


def solution(mesh):
    n_nodes = mesh.shape['node']
    n_ep = mesh.shape['ep']
    row_spec = P(('dp', 'node', 'ep'), None)
    exp_spec = P(('node', 'ep'), None, None)

    def local_layer(tokens, expert_ids, route_w, node_slot, exp_slot, w_gate, w_up, w_down):
        tok_dev, d_model = tokens.shape
        top_k = expert_ids.shape[1]
        d_ff = w_gate.shape[2]
        n_exp = w_gate.shape[0] * n_ep * n_nodes
        limit = max(1, min(top_k, n_nodes // 2))
        cap_node = min(tok_dev, 8 * ((5 * tok_dev * limit + 32 * n_nodes - 1) // (32 * n_nodes)))
        cap_exp = 8 * ((5 * n_nodes * tok_dev * top_k + 32 * n_exp - 1) // (32 * n_exp))
        n_chunks = cap_exp // BLK
        rows = n_ep * BLK

        cube = (SIDE, SIDE, SIDE, BLK, d_model)
        bf16, f32, i32 = jnp.bfloat16, jnp.float32, jnp.int32
        any_spec = pl.BlockSpec(memory_space=pl.ANY)
        dma = pltpu.SemaphoreType.DMA
        out, _, _ = pl.pallas_call(
            functools.partial(moe_kernel, n_chunks),
            name="moe_layer",
            out_shape=(jax.ShapeDtypeStruct((tok_dev, d_model), bf16),
                       jax.ShapeDtypeStruct((n_chunks,) + cube, bf16),
                       jax.ShapeDtypeStruct((n_chunks,) + cube, bf16)),
            in_specs=[any_spec] * 8,
            out_specs=(pl.BlockSpec(memory_space=pltpu.VMEM), any_spec, any_spec),
            scratch_shapes=[
                pltpu.VMEM((top_k, tok_dev), i32), pltpu.VMEM((top_k, tok_dev), f32),
                pltpu.VMEM((top_k, tok_dev), i32), pltpu.VMEM((top_k, tok_dev), i32),
                pltpu.VMEM((tok_dev, d_model), bf16),
                pltpu.VMEM((2, cap_node, tok_dev), bf16),
                *[pltpu.VMEM((SIDE, 2, cap_node, width), bf16) for _, width in part_columns(d_model)],
                pltpu.VMEM((2, top_k, tok_dev), f32), pltpu.VMEM((3, SIDE, 2, top_k, tok_dev), f32), pltpu.VMEM((top_k, tok_dev), f32),
                pltpu.VMEM((2, cap_node, 128), f32), pltpu.VMEM((cap_node, 128), f32),
                pltpu.VMEM((cap_node, d_model), bf16), pltpu.VMEM((cap_node, d_model), bf16),
                pltpu.VMEM((d_model, d_ff), bf16), pltpu.VMEM((d_model, d_ff), bf16), pltpu.VMEM((d_ff, d_model), bf16),
                pltpu.VMEM((2,) + cube, bf16),
                pltpu.VMEM((n_chunks,) + cube, bf16), pltpu.VMEM((n_chunks,) + cube, bf16), pltpu.VMEM((n_chunks,) + cube, bf16),
                pltpu.VMEM((rows, d_ff), bf16),
                pltpu.VMEM((2, cap_node, d_model), f32),
                dma((5,)), dma((3,)), dma((5, 2, 3)), dma((5, 2, 3, 3)), dma((5, n_chunks, 3, 3)), dma((6,)), dma((6,)),
                dma((3, 2, 2)), dma((3, 2, 2)), dma((3, 2, 2)), dma((3, 2, 2)), dma((3, 3)), dma((3, 3)),
            ],
            compiler_params=pltpu.CompilerParams(collective_id=0, has_side_effects=True, vmem_limit_bytes=63 * 2**20),
        )(expert_ids.T, route_w.T, node_slot.T, exp_slot.T, tokens, w_gate[0], w_up[0], w_down[0])
        return out

    return jax.shard_map(local_layer, mesh=mesh, in_specs=(row_spec,) * 5 + (exp_spec,) * 3, out_specs=row_spec, check_vma=False)
```

time: 256 us -> 231 us (0.902)
  Pallas kernels: 251 us -> 229 us
    pallas_call x1, Pallas kernels: 251 us -> 229 us  [local_layer(): pl.pallas_call(functools.partial(moe_kernel, n_chunks), name='moe_layer',...]
where the time goes in v2:
time: 231 us
  Pallas kernels  229 us (99%)
    pallas_call x1, Pallas kernels, local_layer(): pl.pallas_call(functools.partial(moe_kernel, n_chunks), name='moe_layer',...  229 us

profile of v2, /device:TPU:1, one launch (start us, length us, event | category | flops | bytes accessed | tf_op | source)
XLA Modules:
  0.0 231.2 jit_solution(11406878073924933549)
XLA Ops:
  0.0 228.9 %moe_layer.1 = (bf16[256,2048]{1,0:T(8,128)(2,1)}, bf16[5,4,4,4,8,2048]{5,4,3,2,1,0:T(8,128)(2,1)}, bf16[5,4,4,4,8,2048]{5,4,3,2,1,0:T(8,128)(2,1)}) custom-call(s32[8,256]{1,0:T(8,128)} %bitcast.10, f32[8,256]{1,0:T(8,128)} %bitcast.11, s32[8,256]{1,0:T(8,128)} %bitcast.12, s32[8,256]{1,0:T(8,128)} %bitcast.13, bf16[256,2048]{1,0:T(8,128)(2,1)} %tok_hbm.1, ...), custom_call_target="tpu_custom_call" | custom-call | tf_op jit(solution)/shard_map/moe_layer/pallas_call | solution.py:312
  228.9 2.3 copy.10

commit v3 on v2

--- a/solution.py
+++ b/solution.py
@@ -30,8 +30,8 @@
 
 
 def moe_kernel(n_chunks, ids_hbm, rw_hbm, ns_hbm, es_hbm, tok_hbm, wg_hbm, wu_hbm, wd_hbm, out_ref, mid_d, mid_r,
-               ids, rw, ns, es, tok, pick, rg0, rg1, rg2, own_codes, codes, c_send, feat, f_send, r_send, p_recv,
-               wg, wu, wd, send1, hop, work, back, hid, acc,
+               ids, rw, ns, es, tok, pick, rg0, rg1, rg2, own_codes, codes, c_send, feat, f_send, p_buf, p_recv,
+               wg, wu, wd, send1, hop, work, back, hid, acc, lhs,
                in_sem, w_sem, own_sem, send_sem, recv_sem, pair_send, pair_recv, a_send, a_recv, b_send, b_recv, c_ssem, c_rsem):
     f32, bf16 = jnp.float32, jnp.bfloat16
     tok_dev, d_model = tok_hbm.shape
@@ -74,10 +74,15 @@
     for c in inputs:
         c.wait()
 
+    def on_group(m):
+        return (ids[...] >= m * n_ep) & (ids[...] < (m + 1) * n_ep)
+
+    def find_rows(m):
+        slot = jnp.max(jnp.where(on_group(m), ns[...], -1), axis=0, keepdims=True)
+        pick[m] = jnp.where(lax.broadcasted_iota(jnp.int32, (tok_dev, tok_dev), 0) == slot, 1.0, 0.0).astype(bf16)
+
     def route(m):
-        on = (ids[...] >= m * n_ep) & (ids[...] < (m + 1) * n_ep)
-        slot = jnp.max(jnp.where(on, ns[...], -1), axis=0, keepdims=True)
-        kept = on & (ns[...] >= 0) & (es[...] >= 0)
+        kept = on_group(m) & (ns[...] >= 0) & (es[...] >= 0)
         a = jnp.where(kept, (ids[...] - m * n_ep) * SLOTS, 0).astype(f32)
         b = jnp.where(kept, es[...] + 1, 0).astype(f32)
         w = jnp.where(kept, rw[...], 0.0)
@@ -86,17 +91,15 @@
         w3 = w - w1 - w2
         fill = jnp.zeros((128 - 2 * top_k, tok_dev), f32)
         parts = [jnp.concatenate([p, q, fill], axis=0).astype(bf16) for p, q in ((a, w1), (b, w2), (jnp.zeros_like(a), w3))]
-        hot = jnp.where(lax.broadcasted_iota(jnp.int32, (tok_dev, tok_dev), 0) == slot, 1.0, 0.0).astype(bf16)
-        pick[m] = hot[:cap]
-        code = sum(lax.dot_general(p, hot, NT, preferred_element_type=f32) for p in parts[:2])[:top_k]
-        by_row = sum(lax.dot_general(hot[:cap], p, NT, preferred_element_type=f32) for p in parts[::-1])
+        code = sum(lax.dot_general(p, pick[m], NT, preferred_element_type=f32) for p in parts[:2])[:top_k]
+        by_row = sum(lax.dot_general(pick[m, :cap], p, NT, preferred_element_type=f32) for p in parts[::-1])
         return code, by_row
 
-    own_code, own_feat = route(node)
+    find_rows(node)
     for part in range(3):
         c0, width = cols[part]
         rings[part][pos[ROUTES[part][0]], node] = jnp.dot(
-            pick[node], tok[:, c0:c0 + width], preferred_element_type=f32).astype(bf16)
+            pick[node, :cap], tok[:, c0:c0 + width], preferred_element_type=f32).astype(bf16)
     pl.semaphore_wait(barrier, 1 + 3 * len(SHIFTS))
 
     def ring_copies(part, n):
@@ -113,17 +116,20 @@
     for part in range(3):
         for c in ring_copies(part, node)[0]:
             c.start()
+    find_rows(other)
+    p_buf[other] = jnp.dot(pick[other, :cap], tok[...], preferred_element_type=f32).astype(bf16)
+    pair = [to_pair(p_buf.at[other, :, pl.ds(*cols[part])], rings[part].at[pos[ROUTES[part][0]], node], part) for part in range(3)]
+    for c in pair:
+        c.start()
+    far_code, far_feat = route(other)
+    c_send[...] = far_code
+    f_send[...] = far_feat
+    pair_codes = [to_pair(c_send, own_codes.at[node], 3), to_pair(f_send, feat.at[node], 4)]
+    for c in pair_codes:
+        c.start()
+    own_code, own_feat = route(node)
     own_codes[node] = own_code
     feat[node] = own_feat
-    far_code, far_feat = route(other)
-    r_send[...] = jnp.dot(pick[other], tok[...], preferred_element_type=f32).astype(bf16)
-    c_send[...] = far_code
-    f_send[...] = far_feat
-    pair = [to_pair(r_send.at[:, pl.ds(*cols[part])], rings[part].at[pos[ROUTES[part][0]], node], part) for part in range(3)]
-    pair.append(to_pair(c_send, own_codes.at[node], 3))
-    pair.append(to_pair(f_send, feat.at[node], 4))
-    for c in pair:
-        c.start()
     for c in weights:
         c.start()
     acc[...] = jnp.zeros_like(acc)
@@ -132,6 +138,8 @@
     for part in range(3):
         for c in ring_copies(part, other)[0]:
             c.start()
+    for c in pair_codes:
+        c.wait()
     code_copies = [to_ep(own_codes, codes.at[dim, pos[dim]], c_ssem.at[dim, v], c_rsem.at[dim, v], dim, shift)
                    for dim in range(3) for v, shift in enumerate(SHIFTS)]
     for c in code_copies:
@@ -184,16 +192,29 @@
         for c in local:
             c.wait()
 
+    def first_leg(chunk, part, k):
+        ring, dim = ROUTES[part][0], ROUTES[part][1]
+        c0, width = cols[part]
+
+        def line(ref, slot, index):
+            idx = [slot, slice(None), slice(None), slice(None), slice(None), pl.ds(c0, width)]
+            idx[1 + ring], idx[1 + dim] = k, index
+            return ref.at[tuple(idx)]
+
+        for v, shift in enumerate(SHIFTS):
+            to_ep(line(send1, chunk % 2, (pos[dim] + shift) % SIDE), line(mid_d, chunk, pos[dim]),
+                  send_sem.at[0, chunk % 2, part, v], recv_sem.at[0, chunk, part, v], dim, shift).start()
+        pltpu.make_async_copy(line(send1, chunk % 2, pos[dim]), line(mid_d, chunk, pos[dim]), own_sem.at[0, chunk % 2, part]).start()
+
     def gather(chunk):
         for v in (0, 3, 1, 2):
-            if v == 2:
-                @pl.when(chunk == 0)
-                def _():
-                    for n in (node, other):
-                        for part in range(3):
+            for part in range(3):
+                if v == 2:
+                    @pl.when(chunk == 0)
+                    def _():
+                        for n in (node, other):
                             for c in ring_copies(part, n)[1]:
                                 c.wait()
-            for part in range(3):
                 dim = ROUTES[part][0]
                 k = (pos[dim] + v) % SIDE
                 c0, width = cols[part]
@@ -211,6 +232,7 @@
                 idx = [chunk % 2, slice(None), slice(None), slice(None), slice(None), slice(c0, c0 + width)]
                 idx[1 + dim] = k
                 send1[tuple(idx)] = block.reshape(SIDE, SIDE, BLK, width).astype(bf16)
+                first_leg(chunk, part, k)
 
     def ffn(chunk):
         width = 256
@@ -233,37 +255,39 @@
 
         lax.fori_loop(0, d_model // width, down, 0)
 
-    def combine(chunk):
+    def mix(chunk):
         lane = lax.broadcasted_iota(jnp.int32, (cap, rows), 1)
         want = ((lane >> 3) * SLOTS + (lane & 7) + chunk * BLK + 1).astype(f32)
-        width = 512
         for n in range(2):
-            mix = jnp.zeros((cap, rows), f32)
+            w = jnp.zeros((cap, rows), f32)
             for j in range(top_k):
-                mix = jnp.where(feat[n, :, j:j + 1] == want, feat[n, :, top_k + j:top_k + j + 1], mix)
-            hi = mix.astype(bf16)
-            rest = mix - hi.astype(f32)
+                w = jnp.where(feat[n, :, j:j + 1] == want, feat[n, :, top_k + j:top_k + j + 1], w)
+            hi = w.astype(bf16)
+            rest = w - hi.astype(f32)
             mid = rest.astype(bf16)
             lo = (rest - mid.astype(f32)).astype(bf16)
-            for q in range(d_model // width):
-                at = slice(q * width, (q + 1) * width)
-                y = back[chunk, :, :, :, :, at].reshape(rows, width)
-                add = jnp.dot(lo, y, preferred_element_type=f32)
-                add = add + jnp.dot(mid, y, preferred_element_type=f32)
-                add = add + jnp.dot(hi, y, preferred_element_type=f32)
-                acc[n, :, at] += add
+            for i, term in enumerate((lo, mid, hi)):
+                lhs[(2 * i + n) * cap:(2 * i + n + 1) * cap, :] = term
+
+    def mixed(chunk, at):
+        y = back[chunk, :, :, :, :, at].reshape(rows, at.stop - at.start)
+        add = jnp.dot(lhs[...], y, preferred_element_type=f32)
+        return acc[:, at] + (add[:2 * cap] + add[2 * cap:4 * cap] + add[4 * cap:])
+
+    spans = [slice(q, q + 512) for q in range(0, d_model, 512)]
 
     def step(t, carry):
         @pl.when(t < n_chunks)
         def _():
             gather(t)
-            launch(0, t)
 
         for stage in range(1, 6):
             chunk = t - stage
 
-            @pl.when((chunk >= 0) & (chunk < n_chunks))
+            @pl.when((chunk >= 0) & (chunk < (n_chunks if stage < 5 else n_chunks - 1)))
             def _():
+                if stage == 5:
+                    mix(chunk)
                 finish(stage - 1, chunk)
                 if stage == 2:
                     @pl.when(chunk == 0)
@@ -274,18 +298,25 @@
                 if stage < 5:
                     launch(stage, chunk)
                 else:
-                    combine(chunk)
+                    for at in spans:
+                        acc[:, at] = mixed(chunk, at)
         return carry
 
-    lax.fori_loop(0, n_chunks + 5, step, 0)
-
-    r_send[...] = acc[other].astype(bf16)
-    share = to_pair(r_send, p_recv, 5)
-    share.start()
-    mine = lax.dot_general(pick[node], acc[node].astype(bf16), TN, preferred_element_type=f32)
-    share.wait()
-    theirs = lax.dot_general(pick[other], p_recv[...], TN, preferred_element_type=f32)
-    out_ref[...] = (mine + theirs).astype(bf16)
+    lax.fori_loop(0, n_chunks + 4, step, 0)
+
+    last = n_chunks - 1
+    mix(last)
+    finish(4, last)
+    share = []
+    for i, at in enumerate(spans):
+        p_buf[:, :, at] = mixed(last, at).reshape(2, cap, at.stop - at.start).astype(bf16)
+        share.append(to_pair(p_buf.at[other, :, pl.ds(at.start, at.stop - at.start)], p_recv.at[:, pl.ds(at.start, at.stop - at.start)], 5 + i))
+        share[-1].start()
+    for c, at in zip(share, spans):
+        mine = lax.dot_general(pick[node, :cap], p_buf[node, :, at], TN, preferred_element_type=f32)
+        c.wait()
+        theirs = lax.dot_general(pick[other, :cap], p_recv[:, at], TN, preferred_element_type=f32)
+        out_ref[:, at] = (mine + theirs).astype(bf16)
 
 
 def solution(mesh):
@@ -321,17 +352,18 @@
                 pltpu.VMEM((top_k, tok_dev), i32), pltpu.VMEM((top_k, tok_dev), f32),
                 pltpu.VMEM((top_k, tok_dev), i32), pltpu.VMEM((top_k, tok_dev), i32),
                 pltpu.VMEM((tok_dev, d_model), bf16),
-                pltpu.VMEM((2, cap_node, tok_dev), bf16),
+                pltpu.VMEM((2, tok_dev, tok_dev), bf16),
                 *[pltpu.VMEM((SIDE, 2, cap_node, width), bf16) for _, width in part_columns(d_model)],
                 pltpu.VMEM((2, top_k, tok_dev), f32), pltpu.VMEM((3, SIDE, 2, top_k, tok_dev), f32), pltpu.VMEM((top_k, tok_dev), f32),
                 pltpu.VMEM((2, cap_node, 128), f32), pltpu.VMEM((cap_node, 128), f32),
-                pltpu.VMEM((cap_node, d_model), bf16), pltpu.VMEM((cap_node, d_model), bf16),
+                pltpu.VMEM((2, cap_node, d_model), bf16), pltpu.VMEM((cap_node, d_model), bf16),
                 pltpu.VMEM((d_model, d_ff), bf16), pltpu.VMEM((d_model, d_ff), bf16), pltpu.VMEM((d_ff, d_model), bf16),
                 pltpu.VMEM((2,) + cube, bf16),
                 pltpu.VMEM((n_chunks,) + cube, bf16), pltpu.VMEM((n_chunks,) + cube, bf16), pltpu.VMEM((n_chunks,) + cube, bf16),
                 pltpu.VMEM((rows, d_ff), bf16),
-                pltpu.VMEM((2, cap_node, d_model), f32),
-                dma((5,)), dma((3,)), dma((5, 2, 3)), dma((5, 2, 3, 3)), dma((5, n_chunks, 3, 3)), dma((6,)), dma((6,)),
+                pltpu.VMEM((2 * cap_node, d_model), f32),
+                pltpu.VMEM((6 * cap_node, rows), bf16),
+                dma((5,)), dma((3,)), dma((5, 2, 3)), dma((5, 2, 3, 3)), dma((5, n_chunks, 3, 3)), dma((9,)), dma((9,)),
                 dma((3, 2, 2)), dma((3, 2, 2)), dma((3, 2, 2)), dma((3, 2, 2)), dma((3, 3)), dma((3, 3)),
             ],
             compiler_params=pltpu.CompilerParams(collective_id=0, has_side_effects=True, vmem_limit_bytes=63 * 2**20),

time: 231 us -> 225 us (0.974)
  Pallas kernels: 229 us -> 223 us
    pallas_call x1, Pallas kernels: 229 us -> 223 us  [local_layer(): pl.pallas_call(functools.partial(moe_kernel, n_chunks), name='moe_layer',...]
where the time goes in v3:
time: 225 us
  Pallas kernels  223 us (99%)
  local copies, waits for them, and re-layouts  2.3 us (1%)
    pallas_call x1, Pallas kernels, local_layer(): pl.pallas_call(functools.partial(moe_kernel, n_chunks), name='moe_layer',...  223 us

profile of v3, /device:TPU:1, one launch (start us, length us, event | category | flops | bytes accessed | tf_op | source)
XLA Modules:
  0.0 225.3 jit_solution(8950928716054663655)
XLA Ops:
  0.0 223.0 %moe_layer.1 = (bf16[256,2048]{1,0:T(8,128)(2,1)}, bf16[5,4,4,4,8,2048]{5,4,3,2,1,0:T(8,128)(2,1)}, bf16[5,4,4,4,8,2048]{5,4,3,2,1,0:T(8,128)(2,1)}) custom-call(s32[8,256]{1,0:T(8,128)} %bitcast.10, f32[8,256]{1,0:T(8,128)} %bitcast.11, s32[8,256]{1,0:T(8,128)} %bitcast.12, s32[8,256]{1,0:T(8,128)} %bitcast.13, bf16[256,2048]{1,0:T(8,128)(2,1)} %tok_hbm.1, ...), custom_call_target="tpu_custom_call" | custom-call | tf_op jit(solution)/shard_map/moe_layer/pallas_call | solution.py:343
  223.0 2.3 %copy.10 = bf16[256,2048]{1,0:T(8,128)(2,1)} copy(bf16[256,2048]{1,0:T(8,128)(2,1)} %get-tuple-element.6) | data formatting | bytes 2097152

commit v4 on v3

--- a/solution.py
+++ b/solution.py
@@ -29,24 +29,25 @@
     return cols
 
 
-def moe_kernel(n_chunks, ids_hbm, rw_hbm, ns_hbm, es_hbm, tok_hbm, wg_hbm, wu_hbm, wd_hbm, out_ref, mid_d, mid_r,
-               ids, rw, ns, es, tok, pick, rg0, rg1, rg2, own_codes, codes, c_send, feat, f_send, p_buf, p_recv,
-               wg, wu, wd, send1, hop, work, back, hid, acc, lhs,
-               in_sem, w_sem, own_sem, send_sem, recv_sem, pair_send, pair_recv, a_send, a_recv, b_send, b_recv, c_ssem, c_rsem):
+def moe_kernel(n_chunks, ids_hbm, rw_hbm, ns_hbm, es_hbm, tok_hbm, wg_hbm, wu_hbm, wd_hbm, out_ref, mid_d, hop,
+               ids, rw, ns, es, tok, pick, rg0, rg1, rg2, own_codes, codes, c_send, p_buf, p_recv,
+               wg, wu, wd, send1, work, mid_r, hid, acc0, acc1, acc2, far0, far1, far2, near0, near1, near2,
+               in_sem, w_sem, own_sem, send_sem, recv_sem, pair_send, pair_recv, a_send, a_recv, b_send, b_recv, c_ssem, c_rsem,
+               f_send, f_recv, n_send, n_recv):
     f32, bf16 = jnp.float32, jnp.bfloat16
     tok_dev, d_model = tok_hbm.shape
     d_ff = wg_hbm.shape[1]
     top_k = ids_hbm.shape[0]
     n_ep = SIDE ** 3
     rows = n_ep * BLK
-    cap = feat.shape[1]
+    cap = p_recv.shape[0]
     half = cap // 2
     node = lax.axis_index("node")
     other = 1 - node
     ep = lax.axis_index("ep")
     pos = (ep // (SIDE * SIDE), (ep // SIDE) % SIDE, ep % SIDE)
     cols = part_columns(d_model)
-    rings = (rg0, rg1, rg2)
+    rings, accs, fars, nears = (rg0, rg1, rg2), (acc0, acc1, acc2), (far0, far1, far2), (near0, near1, near2)
 
     def peer(dim, shift):
         at = [pos[0], pos[1], pos[2]]
@@ -89,11 +90,8 @@
         w1 = w.astype(bf16).astype(f32)
         w2 = (w - w1).astype(bf16).astype(f32)
         w3 = w - w1 - w2
-        fill = jnp.zeros((128 - 2 * top_k, tok_dev), f32)
-        parts = [jnp.concatenate([p, q, fill], axis=0).astype(bf16) for p, q in ((a, w1), (b, w2), (jnp.zeros_like(a), w3))]
-        code = sum(lax.dot_general(p, pick[m], NT, preferred_element_type=f32) for p in parts[:2])[:top_k]
-        by_row = sum(lax.dot_general(pick[m, :cap], p, NT, preferred_element_type=f32) for p in parts[::-1])
-        return code, by_row
+        parts = [jnp.concatenate([p, q], axis=0).astype(bf16) for p, q in ((a, w1), (b, w2), (jnp.zeros_like(a), w3))]
+        return sum(lax.dot_general(p, pick[m], NT, preferred_element_type=f32) for p in parts[::-1])
 
     find_rows(node)
     for part in range(3):
@@ -121,25 +119,20 @@
     pair = [to_pair(p_buf.at[other, :, pl.ds(*cols[part])], rings[part].at[pos[ROUTES[part][0]], node], part) for part in range(3)]
     for c in pair:
         c.start()
-    far_code, far_feat = route(other)
-    c_send[...] = far_code
-    f_send[...] = far_feat
-    pair_codes = [to_pair(c_send, own_codes.at[node], 3), to_pair(f_send, feat.at[node], 4)]
-    for c in pair_codes:
-        c.start()
-    own_code, own_feat = route(node)
-    own_codes[node] = own_code
-    feat[node] = own_feat
+    c_send[...] = route(other)
+    pair_codes = to_pair(c_send, own_codes.at[node], 3)
+    pair_codes.start()
+    own_codes[node] = route(node)
     for c in weights:
         c.start()
-    acc[...] = jnp.zeros_like(acc)
+    for acc in accs:
+        acc[...] = jnp.zeros_like(acc)
     for c in pair:
         c.wait()
     for part in range(3):
         for c in ring_copies(part, other)[0]:
             c.start()
-    for c in pair_codes:
-        c.wait()
+    pair_codes.wait()
     code_copies = [to_ep(own_codes, codes.at[dim, pos[dim]], c_ssem.at[dim, v], c_rsem.at[dim, v], dim, shift)
                    for dim in range(3) for v, shift in enumerate(SHIFTS)]
     for c in code_copies:
@@ -155,7 +148,7 @@
     for c in code_copies:
         c.wait()
 
-    stages = ((send1, mid_d, 1), (mid_d, work, 2), (work, hop, 2), (hop, mid_r, 1), (mid_r, back, 0))
+    stages = ((send1, mid_d, 1), (mid_d, work, 2), (work, hop, 2), (hop, mid_r, 1))
 
     def plane(ref, chunk, dim, index, part):
         c0, width = cols[part]
@@ -206,6 +199,12 @@
                   send_sem.at[0, chunk % 2, part, v], recv_sem.at[0, chunk, part, v], dim, shift).start()
         pltpu.make_async_copy(line(send1, chunk % 2, pos[dim]), line(mid_d, chunk, pos[dim]), own_sem.at[0, chunk % 2, part]).start()
 
+    def plane_codes(chunk, dim):
+        o0, o1 = [d for d in range(3) if d != dim]
+        r = lax.broadcasted_iota(jnp.int32, (SIDE * SIDE * BLK, cap), 0)
+        expert = pos[dim] * STRIDE[dim] + (r >> 5) * STRIDE[o0] + ((r >> 3) & 3) * STRIDE[o1]
+        return (expert * SLOTS + (r & 7) + chunk * BLK + 1).astype(f32)
+
     def gather(chunk):
         for v in (0, 3, 1, 2):
             for part in range(3):
@@ -218,10 +217,7 @@
                 dim = ROUTES[part][0]
                 k = (pos[dim] + v) % SIDE
                 c0, width = cols[part]
-                o0, o1 = [d for d in range(3) if d != dim]
-                r = lax.broadcasted_iota(jnp.int32, (SIDE * SIDE * BLK, cap), 0)
-                expert = pos[dim] * STRIDE[dim] + (r >> 5) * STRIDE[o0] + ((r >> 3) & 3) * STRIDE[o1]
-                want = (expert * SLOTS + (r & 7) + chunk * BLK + 1).astype(f32)
+                want = plane_codes(chunk, dim)
                 block = None
                 for n in range(2):
                     hit = jnp.zeros(want.shape, f32)
@@ -255,39 +251,36 @@
 
         lax.fori_loop(0, d_model // width, down, 0)
 
-    def mix(chunk):
-        lane = lax.broadcasted_iota(jnp.int32, (cap, rows), 1)
-        want = ((lane >> 3) * SLOTS + (lane & 7) + chunk * BLK + 1).astype(f32)
+    def fold(chunk, v, part):
+        dim = ROUTES[part][0]
+        k = (pos[dim] + v) % SIDE
+        c0, width = cols[part]
+        want = plane_codes(chunk, dim)
+        idx = [chunk, slice(None), slice(None), slice(None), slice(None), slice(c0, c0 + width)]
+        idx[1 + dim] = k
+        y = mid_r[tuple(idx)].reshape(SIDE * SIDE * BLK, width)
+        y = jnp.concatenate([y, y, y], axis=0)
         for n in range(2):
-            w = jnp.zeros((cap, rows), f32)
+            w = jnp.zeros(want.shape, f32)
             for j in range(top_k):
-                w = jnp.where(feat[n, :, j:j + 1] == want, feat[n, :, top_k + j:top_k + j + 1], w)
+                w = jnp.where(codes[dim, k, n, j:j + 1, :cap] == want, codes[dim, k, n, top_k + j:top_k + j + 1, :cap], w)
             hi = w.astype(bf16)
             rest = w - hi.astype(f32)
             mid = rest.astype(bf16)
             lo = (rest - mid.astype(f32)).astype(bf16)
-            for i, term in enumerate((lo, mid, hi)):
-                lhs[(2 * i + n) * cap:(2 * i + n + 1) * cap, :] = term
-
-    def mixed(chunk, at):
-        y = back[chunk, :, :, :, :, at].reshape(rows, at.stop - at.start)
-        add = jnp.dot(lhs[...], y, preferred_element_type=f32)
-        return acc[:, at] + (add[:2 * cap] + add[2 * cap:4 * cap] + add[4 * cap:])
-
-    spans = [slice(q, q + 512) for q in range(0, d_model, 512)]
+            terms = jnp.concatenate([lo, mid, hi], axis=0)
+            accs[part][k, n] += lax.dot_general(terms, y, TN, preferred_element_type=f32)
 
     def step(t, carry):
         @pl.when(t < n_chunks)
         def _():
             gather(t)
 
-        for stage in range(1, 6):
+        for stage in range(1, 5):
             chunk = t - stage
 
-            @pl.when((chunk >= 0) & (chunk < (n_chunks if stage < 5 else n_chunks - 1)))
+            @pl.when((chunk >= 0) & (chunk < (n_chunks if stage < 4 else n_chunks - 1)))
             def _():
-                if stage == 5:
-                    mix(chunk)
                 finish(stage - 1, chunk)
                 if stage == 2:
                     @pl.when(chunk == 0)
@@ -295,28 +288,66 @@
                         for c in weights:
                             c.wait()
                     ffn(chunk)
-                if stage < 5:
+                if stage < 4:
                     launch(stage, chunk)
                 else:
-                    for at in spans:
-                        acc[:, at] = mixed(chunk, at)
+                    for v in range(SIDE):
+                        for part in range(3):
+                            fold(chunk, v, part)
         return carry
 
-    lax.fori_loop(0, n_chunks + 4, step, 0)
+    lax.fori_loop(0, n_chunks + 3, step, 0)
+
+    def far_copies(part, n):
+        dim = ROUTES[part][0]
+        k = (pos[dim] + 2) % SIDE
+        return [to_ep(accs[part].at[k, n, pl.ds(v * half, half)], fars[part].at[v, n], f_send.at[part, n, v], f_recv.at[part, n, v],
+                      dim, (1, 3)[v]) for v in range(2)]
+
+    def near_copies(part, n):
+        dim = ROUTES[part][0]
+        return [to_ep(accs[part].at[(pos[dim] + (1, 3)[v]) % SIDE, n], nears[part].at[v, n], n_send.at[part, n, v], n_recv.at[part, n, v],
+                      dim, (1, 3)[v]) for v in range(2)]
 
     last = n_chunks - 1
-    mix(last)
-    finish(4, last)
+    finish(3, last)
+    for part in range(3):
+        fold(last, 2, part)
+        for c in far_copies(part, other):
+            c.start()
+    for part in range(3):
+        for c in far_copies(part, node):
+            c.start()
+    for v in (1, 3, 0):
+        for part in range(3):
+            fold(last, v, part)
+    for n in (other, node):
+        for part in range(3):
+            i = pos[ROUTES[part][0]]
+            for v, c in enumerate(far_copies(part, n)):
+                c.wait()
+                accs[part][(i + (1, 3)[v]) % SIDE, n, v * half:(v + 1) * half] += fars[part][v, n]
+            for c in near_copies(part, n):
+                c.start()
+
+    def total(part, n):
+        for c in near_copies(part, n):
+            c.wait()
+        return (accs[part][pos[ROUTES[part][0]], n] + nears[part][0, n] + nears[part][1, n]).astype(bf16)
+
+    spans = [slice(c0, c0 + width) for c0, width in cols]
     share = []
-    for i, at in enumerate(spans):
-        p_buf[:, :, at] = mixed(last, at).reshape(2, cap, at.stop - at.start).astype(bf16)
-        share.append(to_pair(p_buf.at[other, :, pl.ds(at.start, at.stop - at.start)], p_recv.at[:, pl.ds(at.start, at.stop - at.start)], 5 + i))
+    for part, at in enumerate(spans):
+        p_buf[other, :, at] = total(part, other)
+        share.append(to_pair(p_buf.at[other, :, pl.ds(*cols[part])], p_recv.at[:, pl.ds(*cols[part])], 4 + part))
         share[-1].start()
-    for c, at in zip(share, spans):
-        mine = lax.dot_general(pick[node, :cap], p_buf[node, :, at], TN, preferred_element_type=f32)
+    for c in share:
         c.wait()
-        theirs = lax.dot_general(pick[other, :cap], p_recv[:, at], TN, preferred_element_type=f32)
-        out_ref[:, at] = (mine + theirs).astype(bf16)
+    for at in spans:
+        out_ref[:, at] = lax.dot_general(pick[other, :cap], p_recv[:, at], TN, preferred_element_type=f32).astype(bf16)
+    for part, at in enumerate(spans):
+        mine = lax.dot_general(pick[node, :cap], total(part, node), TN, preferred_element_type=f32)
+        out_ref[:, at] = (out_ref[:, at].astype(f32) + mine).astype(bf16)
 
 
 def solution(mesh):
@@ -354,19 +385,19 @@
                 pltpu.VMEM((tok_dev, d_model), bf16),
                 pltpu.VMEM((2, tok_dev, tok_dev), bf16),
                 *[pltpu.VMEM((SIDE, 2, cap_node, width), bf16) for _, width in part_columns(d_model)],
-                pltpu.VMEM((2, top_k, tok_dev), f32), pltpu.VMEM((3, SIDE, 2, top_k, tok_dev), f32), pltpu.VMEM((top_k, tok_dev), f32),
-                pltpu.VMEM((2, cap_node, 128), f32), pltpu.VMEM((cap_node, 128), f32),
+                pltpu.VMEM((2, 2 * top_k, tok_dev), f32), pltpu.VMEM((3, SIDE, 2, 2 * top_k, tok_dev), f32), pltpu.VMEM((2 * top_k, tok_dev), f32),
                 pltpu.VMEM((2, cap_node, d_model), bf16), pltpu.VMEM((cap_node, d_model), bf16),
                 pltpu.VMEM((d_model, d_ff), bf16), pltpu.VMEM((d_model, d_ff), bf16), pltpu.VMEM((d_ff, d_model), bf16),
-                pltpu.VMEM((2,) + cube, bf16),
-                pltpu.VMEM((n_chunks,) + cube, bf16), pltpu.VMEM((n_chunks,) + cube, bf16), pltpu.VMEM((n_chunks,) + cube, bf16),
+                pltpu.VMEM((2,) + cube, bf16), pltpu.VMEM((n_chunks,) + cube, bf16), pltpu.VMEM((n_chunks,) + cube, bf16),
                 pltpu.VMEM((rows, d_ff), bf16),
-                pltpu.VMEM((2 * cap_node, d_model), f32),
-                pltpu.VMEM((6 * cap_node, rows), bf16),
-                dma((5,)), dma((3,)), dma((5, 2, 3)), dma((5, 2, 3, 3)), dma((5, n_chunks, 3, 3)), dma((9,)), dma((9,)),
+                *[pltpu.VMEM((SIDE, 2, cap_node, width), f32) for _, width in part_columns(d_model)],
+                *[pltpu.VMEM((2, 2, cap_node // 2, width), f32) for _, width in part_columns(d_model)],
+                *[pltpu.VMEM((2, 2, cap_node, width), f32) for _, width in part_columns(d_model)],
+                dma((5,)), dma((3,)), dma((4, 2, 3)), dma((4, 2, 3, 3)), dma((4, n_chunks, 3, 3)), dma((7,)), dma((7,)),
                 dma((3, 2, 2)), dma((3, 2, 2)), dma((3, 2, 2)), dma((3, 2, 2)), dma((3, 3)), dma((3, 3)),
+                dma((3, 2, 2)), dma((3, 2, 2)), dma((3, 2, 2)), dma((3, 2, 2)),
             ],
-            compiler_params=pltpu.CompilerParams(collective_id=0, has_side_effects=True, vmem_limit_bytes=63 * 2**20),
+            compiler_params=pltpu.CompilerParams(collective_id=0, has_side_effects=True, vmem_limit_bytes=67_043_328),
         )(expert_ids.T, route_w.T, node_slot.T, exp_slot.T, tokens, w_gate[0], w_up[0], w_down[0])
         return out
 

time: 225 us -> 220 us (0.978)
  Pallas kernels: 223 us -> 217 us
    pallas_call x1, Pallas kernels: 223 us -> 217 us  [local_layer(): pl.pallas_call(functools.partial(moe_kernel, n_chunks), name='moe_layer',...]
where the time goes in v4:
time: 220 us; the launch traced here: 219 us
  Pallas kernels  217 us (99%)
  local copies, waits for them, and re-layouts  2.3 us (1%)
    pallas_call x1, Pallas kernels, local_layer(): pl.pallas_call(functools.partial(moe_kernel, n_chunks), name='moe_layer',...  217 us

profile of v4, /device:TPU:1, one launch (start us, length us, event | category | flops | bytes accessed | tf_op | source)
XLA Modules:
  0.0 219.2 jit_solution(6134424377768929295)
XLA Ops:
  0.0 216.9 %moe_layer.1 = (bf16[256,2048]{1,0:T(8,128)(2,1)}, bf16[5,4,4,4,8,2048]{5,4,3,2,1,0:T(8,128)(2,1)}, bf16[5,4,4,4,8,2048]{5,4,3,2,1,0:T(8,128)(2,1)}) custom-call(s32[8,256]{1,0:T(8,128)} %bitcast.10, f32[8,256]{1,0:T(8,128)} %bitcast.11, s32[8,256]{1,0:T(8,128)} %bitcast.12, s32[8,256]{1,0:T(8,128)} %bitcast.13, bf16[256,2048]{1,0:T(8,128)(2,1)} %tok_hbm.1, ...), custom_call_target="tpu_custom_call" | custom-call | tf_op jit(solution)/shard_map/moe_layer/pallas_call | solution.py:374
  216.9 2.3 %copy.10 = bf16[256,2048]{1,0:T(8,128)(2,1)} copy(bf16[256,2048]{1,0:T(8,128)(2,1)} %get-tuple-element.6) | data formatting | bytes 2097152

commit v5 on v4

--- a/solution.py
+++ b/solution.py
@@ -19,21 +19,15 @@
 
 
 def part_columns(d_model):
-    tiles = d_model // 128
-    base, extra = tiles // 3, tiles % 3
-    cols, at = [], 0
-    for k in range(3):
-        width = (base + (1 if k >= 3 - extra else 0)) * 128
-        cols.append((at, width))
-        at += width
-    return cols
+    width = d_model // 128 // 3 * 128
+    return [(k * width, width) for k in range(3)]
 
 
 def moe_kernel(n_chunks, ids_hbm, rw_hbm, ns_hbm, es_hbm, tok_hbm, wg_hbm, wu_hbm, wd_hbm, out_ref, mid_d, hop,
-               ids, rw, ns, es, tok, pick, rg0, rg1, rg2, own_codes, codes, c_send, p_buf, p_recv,
+               ids, rw, ns, es, tok, pick, rg0, rg1, rg2, own_codes, codes, c_send, p_buf, p_recv, x_rows, x_send, x_leg, x_back, x_acc,
                wg, wu, wd, send1, work, mid_r, hid, acc0, acc1, acc2, far0, far1, far2, near0, near1, near2,
                in_sem, w_sem, own_sem, send_sem, recv_sem, pair_send, pair_recv, a_send, a_recv, b_send, b_recv, c_ssem, c_rsem,
-               f_send, f_recv, n_send, n_recv):
+               f_send, f_recv, n_send, n_recv, x_ssem, x_rsem, x_osem):
     f32, bf16 = jnp.float32, jnp.bfloat16
     tok_dev, d_model = tok_hbm.shape
     d_ff = wg_hbm.shape[1]
@@ -47,6 +41,7 @@
     ep = lax.axis_index("ep")
     pos = (ep // (SIDE * SIDE), (ep // SIDE) % SIDE, ep % SIDE)
     cols = part_columns(d_model)
+    rest = cols[2][0] + cols[2][1]
     rings, accs, fars, nears = (rg0, rg1, rg2), (acc0, acc1, acc2), (far0, far1, far2), (near0, near1, near2)
 
     def peer(dim, shift):
@@ -98,6 +93,7 @@
         c0, width = cols[part]
         rings[part][pos[ROUTES[part][0]], node] = jnp.dot(
             pick[node, :cap], tok[:, c0:c0 + width], preferred_element_type=f32).astype(bf16)
+    x_rows[node] = jnp.dot(pick[node, :cap], tok[:, rest:], preferred_element_type=f32).astype(bf16)
     pl.semaphore_wait(barrier, 1 + 3 * len(SHIFTS))
 
     def ring_copies(part, n):
@@ -117,6 +113,7 @@
     find_rows(other)
     p_buf[other] = jnp.dot(pick[other, :cap], tok[...], preferred_element_type=f32).astype(bf16)
     pair = [to_pair(p_buf.at[other, :, pl.ds(*cols[part])], rings[part].at[pos[ROUTES[part][0]], node], part) for part in range(3)]
+    pair.append(to_pair(p_buf.at[other, :, pl.ds(rest, d_model - rest)], x_rows.at[node], 7))
     for c in pair:
         c.start()
     c_send[...] = route(other)
@@ -139,15 +136,6 @@
         c.start()
     for dim in range(3):
         codes[dim, pos[dim]] = own_codes[...]
-    for n in (node, other):
-        for part in range(3):
-            first, onward = ring_copies(part, n)
-            for v in range(2):
-                first[v].wait()
-                onward[v].start()
-    for c in code_copies:
-        c.wait()
-
     stages = ((send1, mid_d, 1), (mid_d, work, 2), (work, hop, 2), (hop, mid_r, 1))
 
     def plane(ref, chunk, dim, index, part):
@@ -185,6 +173,86 @@
         for c in local:
             c.wait()
 
+    def plane_codes(chunk, dim, at):
+        o0, o1 = [d for d in range(3) if d != dim]
+        r = lax.broadcasted_iota(jnp.int32, (SIDE * SIDE * BLK, cap), 0)
+        expert = at * STRIDE[dim] + (r >> 5) * STRIDE[o0] + ((r >> 3) & 3) * STRIDE[o1]
+        return (expert * SLOTS + (r & 7) + chunk * BLK + 1).astype(f32)
+
+    def pick_slots(want, code, packed):
+        block = None
+        for n in range(2):
+            hit = jnp.zeros(want.shape, f32)
+            for j in range(top_k):
+                hit = jnp.where(code[n, j:j + 1, :cap] == want, 1.0, hit)
+            got = jnp.dot(hit.astype(bf16), packed[n], preferred_element_type=f32)
+            block = got if block is None else block + got
+        return block.astype(bf16).reshape(SIDE, SIDE, BLK, -1)
+
+    def weigh_slots(want, code, y, n):
+        w = jnp.zeros(want.shape, f32)
+        for j in range(top_k):
+            w = jnp.where(code[n, j:j + 1, :cap] == want, code[n, top_k + j:top_k + j + 1, :cap], w)
+        hi = w.astype(bf16)
+        left = w - hi.astype(f32)
+        mid = left.astype(bf16)
+        lo = (left - mid.astype(f32)).astype(bf16)
+        return lax.dot_general(jnp.concatenate([lo, mid, hi], axis=0), jnp.concatenate([y, y, y], axis=0), TN, preferred_element_type=f32)
+
+    x_stages = ((x_send, x_leg), (x_leg, mid_d), (mid_d, work), (work, hop), (hop, mid_r), (mid_r, x_back))
+
+    def x_copies(leg, chunk, route_no):
+        src, dst = x_stages[leg]
+        dim = ROUTES[route_no][leg if leg < 3 else 5 - leg]
+
+        def at(ref, index):
+            c0 = 0 if ref.shape[-1] == d_model - rest else rest
+            idx = [chunk % 2 if ref is x_send else chunk, slice(None), slice(None), slice(None), slice(None), pl.ds(c0, d_model - rest)]
+            idx[1 + dim] = index
+            return ref.at[tuple(idx)]
+
+        remote = [to_ep(at(src, (pos[dim] + shift) % SIDE), at(dst, pos[dim]), x_ssem.at[leg, chunk % 2, v], x_rsem.at[leg, chunk, v], dim, shift)
+                  for v, shift in enumerate(SHIFTS)]
+        return remote + [pltpu.make_async_copy(at(src, pos[dim]), at(dst, pos[dim]), x_osem.at[leg, chunk % 2])]
+
+    def x_launch(leg, chunk):
+        for route_no in range(3):
+            @pl.when(chunk % 3 == route_no)
+            def _():
+                for c in x_copies(leg, chunk, route_no):
+                    c.start()
+
+    def x_finish(leg, chunk):
+        for route_no in range(3):
+            @pl.when(chunk % 3 == route_no)
+            def _():
+                for c in x_copies(leg, chunk, route_no):
+                    c.wait()
+
+    def x_gather(chunk):
+        for z in range(SIDE):
+            x_send[chunk % 2, z] = pick_slots(plane_codes(chunk, 0, z), own_codes, x_rows)
+        x_launch(0, chunk)
+
+    def x_combine(chunk):
+        x_finish(5, chunk)
+        for z in range(SIDE):
+            y = x_back[chunk, z].reshape(SIDE * SIDE * BLK, d_model - rest)
+            want = plane_codes(chunk, 0, z)
+            for n in range(2):
+                x_acc[n] += weigh_slots(want, own_codes, y, n)
+
+    x_acc[...] = jnp.zeros_like(x_acc)
+    x_gather(0)
+    for n in (node, other):
+        for part in range(3):
+            first, onward = ring_copies(part, n)
+            for v in range(2):
+                first[v].wait()
+                onward[v].start()
+    for c in code_copies:
+        c.wait()
+
     def first_leg(chunk, part, k):
         ring, dim = ROUTES[part][0], ROUTES[part][1]
         c0, width = cols[part]
@@ -198,12 +266,6 @@
             to_ep(line(send1, chunk % 2, (pos[dim] + shift) % SIDE), line(mid_d, chunk, pos[dim]),
                   send_sem.at[0, chunk % 2, part, v], recv_sem.at[0, chunk, part, v], dim, shift).start()
         pltpu.make_async_copy(line(send1, chunk % 2, pos[dim]), line(mid_d, chunk, pos[dim]), own_sem.at[0, chunk % 2, part]).start()
-
-    def plane_codes(chunk, dim):
-        o0, o1 = [d for d in range(3) if d != dim]
-        r = lax.broadcasted_iota(jnp.int32, (SIDE * SIDE * BLK, cap), 0)
-        expert = pos[dim] * STRIDE[dim] + (r >> 5) * STRIDE[o0] + ((r >> 3) & 3) * STRIDE[o1]
-        return (expert * SLOTS + (r & 7) + chunk * BLK + 1).astype(f32)
 
     def gather(chunk):
         for v in (0, 3, 1, 2):
@@ -217,17 +279,9 @@
                 dim = ROUTES[part][0]
                 k = (pos[dim] + v) % SIDE
                 c0, width = cols[part]
-                want = plane_codes(chunk, dim)
-                block = None
-                for n in range(2):
-                    hit = jnp.zeros(want.shape, f32)
-                    for j in range(top_k):
-                        hit = jnp.where(codes[dim, k, n, j:j + 1, :cap] == want, 1.0, hit)
-                    got = jnp.dot(hit.astype(bf16), rings[part][k, n], preferred_element_type=f32)
-                    block = got if block is None else block + got
                 idx = [chunk % 2, slice(None), slice(None), slice(None), slice(None), slice(c0, c0 + width)]
                 idx[1 + dim] = k
-                send1[tuple(idx)] = block.reshape(SIDE, SIDE, BLK, width).astype(bf16)
+                send1[tuple(idx)] = pick_slots(plane_codes(chunk, dim, pos[dim]), codes.at[dim, k], rings[part].at[k])
                 first_leg(chunk, part, k)
 
     def ffn(chunk):
@@ -255,26 +309,23 @@
         dim = ROUTES[part][0]
         k = (pos[dim] + v) % SIDE
         c0, width = cols[part]
-        want = plane_codes(chunk, dim)
+        want = plane_codes(chunk, dim, pos[dim])
         idx = [chunk, slice(None), slice(None), slice(None), slice(None), slice(c0, c0 + width)]
         idx[1 + dim] = k
         y = mid_r[tuple(idx)].reshape(SIDE * SIDE * BLK, width)
-        y = jnp.concatenate([y, y, y], axis=0)
         for n in range(2):
-            w = jnp.zeros(want.shape, f32)
-            for j in range(top_k):
-                w = jnp.where(codes[dim, k, n, j:j + 1, :cap] == want, codes[dim, k, n, top_k + j:top_k + j + 1, :cap], w)
-            hi = w.astype(bf16)
-            rest = w - hi.astype(f32)
-            mid = rest.astype(bf16)
-            lo = (rest - mid.astype(f32)).astype(bf16)
-            terms = jnp.concatenate([lo, mid, hi], axis=0)
-            accs[part][k, n] += lax.dot_general(terms, y, TN, preferred_element_type=f32)
+            accs[part][k, n] += weigh_slots(want, codes.at[dim, k], y, n)
 
     def step(t, carry):
         @pl.when(t < n_chunks)
         def _():
             gather(t)
+            x_finish(0, t)
+            x_launch(1, t)
+
+        @pl.when(t + 1 < n_chunks)
+        def _():
+            x_gather(t + 1)
 
         for stage in range(1, 5):
             chunk = t - stage
@@ -282,18 +333,25 @@
             @pl.when((chunk >= 0) & (chunk < (n_chunks if stage < 4 else n_chunks - 1)))
             def _():
                 finish(stage - 1, chunk)
+                x_finish(stage, chunk)
                 if stage == 2:
                     @pl.when(chunk == 0)
                     def _():
                         for c in weights:
                             c.wait()
                     ffn(chunk)
+                x_launch(stage + 1, chunk)
                 if stage < 4:
                     launch(stage, chunk)
                 else:
                     for v in range(SIDE):
                         for part in range(3):
                             fold(chunk, v, part)
+
+        @pl.when(t >= 5)
+        def _():
+            x_combine(t - 5)
+
         return carry
 
     lax.fori_loop(0, n_chunks + 3, step, 0)
@@ -318,6 +376,8 @@
     for part in range(3):
         for c in far_copies(part, node):
             c.start()
+    x_finish(4, last)
+    x_launch(5, last)
     for v in (1, 3, 0):
         for part in range(3):
             fold(last, v, part)
@@ -330,6 +390,9 @@
             for c in near_copies(part, n):
                 c.start()
 
+    for chunk in range(max(n_chunks - 2, 0), n_chunks):
+        x_combine(chunk)
+
     def total(part, n):
         for c in near_copies(part, n):
             c.wait()
@@ -341,8 +404,14 @@
         p_buf[other, :, at] = total(part, other)
         share.append(to_pair(p_buf.at[other, :, pl.ds(*cols[part])], p_recv.at[:, pl.ds(*cols[part])], 4 + part))
         share[-1].start()
+    p_buf[other, :, rest:] = x_acc[other].astype(bf16)
+    share.append(to_pair(p_buf.at[other, :, pl.ds(rest, d_model - rest)], p_recv.at[:, pl.ds(rest, d_model - rest)], 8))
+    share[-1].start()
     for c in share:
         c.wait()
+    x_sum = lax.dot_general(pick[other, :cap], p_recv[:, rest:], TN, preferred_element_type=f32)
+    x_sum = x_sum + lax.dot_general(pick[node, :cap], x_acc[node].astype(bf16), TN, preferred_element_type=f32)
+    out_ref[:, rest:] = x_sum.astype(bf16)
     for at in spans:
         out_ref[:, at] = lax.dot_general(pick[other, :cap], p_recv[:, at], TN, preferred_element_type=f32).astype(bf16)
     for part, at in enumerate(spans):
@@ -368,6 +437,8 @@
         rows = n_ep * BLK
 
         cube = (SIDE, SIDE, SIDE, BLK, d_model)
+        wide = d_model - 3 * part_columns(d_model)[0][1]
+        x_cube = (SIDE, SIDE, SIDE, BLK, wide)
         bf16, f32, i32 = jnp.bfloat16, jnp.float32, jnp.int32
         any_spec = pl.BlockSpec(memory_space=pl.ANY)
         dma = pltpu.SemaphoreType.DMA
@@ -387,15 +458,18 @@
                 *[pltpu.VMEM((SIDE, 2, cap_node, width), bf16) for _, width in part_columns(d_model)],
                 pltpu.VMEM((2, 2 * top_k, tok_dev), f32), pltpu.VMEM((3, SIDE, 2, 2 * top_k, tok_dev), f32), pltpu.VMEM((2 * top_k, tok_dev), f32),
                 pltpu.VMEM((2, cap_node, d_model), bf16), pltpu.VMEM((cap_node, d_model), bf16),
+                pltpu.VMEM((2, cap_node, wide), bf16), pltpu.VMEM((2,) + x_cube, bf16), pltpu.VMEM((n_chunks,) + x_cube, bf16),
+                pltpu.VMEM((n_chunks,) + x_cube, bf16), pltpu.VMEM((2, cap_node, wide), f32),
                 pltpu.VMEM((d_model, d_ff), bf16), pltpu.VMEM((d_model, d_ff), bf16), pltpu.VMEM((d_ff, d_model), bf16),
                 pltpu.VMEM((2,) + cube, bf16), pltpu.VMEM((n_chunks,) + cube, bf16), pltpu.VMEM((n_chunks,) + cube, bf16),
                 pltpu.VMEM((rows, d_ff), bf16),
                 *[pltpu.VMEM((SIDE, 2, cap_node, width), f32) for _, width in part_columns(d_model)],
                 *[pltpu.VMEM((2, 2, cap_node // 2, width), f32) for _, width in part_columns(d_model)],
                 *[pltpu.VMEM((2, 2, cap_node, width), f32) for _, width in part_columns(d_model)],
-                dma((5,)), dma((3,)), dma((4, 2, 3)), dma((4, 2, 3, 3)), dma((4, n_chunks, 3, 3)), dma((7,)), dma((7,)),
+                dma((5,)), dma((3,)), dma((4, 2, 3)), dma((4, 2, 3, 3)), dma((4, n_chunks, 3, 3)), dma((9,)), dma((9,)),
                 dma((3, 2, 2)), dma((3, 2, 2)), dma((3, 2, 2)), dma((3, 2, 2)), dma((3, 3)), dma((3, 3)),
                 dma((3, 2, 2)), dma((3, 2, 2)), dma((3, 2, 2)), dma((3, 2, 2)),
+                dma((6, 2, 3)), dma((6, n_chunks, 3)), dma((6, 2)),
             ],
             compiler_params=pltpu.CompilerParams(collective_id=0, has_side_effects=True, vmem_limit_bytes=67_043_328),
         )(expert_ids.T, route_w.T, node_slot.T, exp_slot.T, tokens, w_gate[0], w_up[0], w_down[0])

time: 220 us -> 217 us (0.986)
  Pallas kernels: 217 us -> 213 us
    pallas_call x1, Pallas kernels: 217 us -> 213 us  [local_layer(): pl.pallas_call(functools.partial(moe_kernel, n_chunks), name='moe_layer',...]
where the time goes in v5:
time: 217 us; the launch traced here: 216 us
  Pallas kernels  213 us (98%)
  local copies, waits for them, and re-layouts  2.3 us (1%)
    pallas_call x1, Pallas kernels, local_layer(): pl.pallas_call(functools.partial(moe_kernel, n_chunks), name='moe_layer',...  213 us

profile of v5, /device:TPU:1, one launch (start us, length us, event | category | flops | bytes accessed | tf_op | source)
XLA Modules:
  0.0 215.5 jit_solution(10918625653937641653)
XLA Ops:
  0.0 213.2 %moe_layer.1 = (bf16[256,2048]{1,0:T(8,128)(2,1)}, bf16[5,4,4,4,8,2048]{5,4,3,2,1,0:T(8,128)(2,1)}, bf16[5,4,4,4,8,2048]{5,4,3,2,1,0:T(8,128)(2,1)}) custom-call(s32[8,256]{1,0:T(8,128)} %bitcast.10, f32[8,256]{1,0:T(8,128)} %bitcast.11, s32[8,256]{1,0:T(8,128)} %bitcast.12, s32[8,256]{1,0:T(8,128)} %bitcast.13, bf16[256,2048]{1,0:T(8,128)(2,1)} %tok_hbm.1, ...), custom_call_target="tpu_custom_call" | custom-call | tf_op jit(solution)/shard_map/moe_layer/pallas_call | solution.py:445
  213.2 2.3 %copy.10 = bf16[256,2048]{1,0:T(8,128)(2,1)} copy(bf16[256,2048]{1,0:T(8,128)(2,1)} %get-tuple-element.6) | data formatting | bytes 2097152

commit v6 on v5

--- a/solution.py
+++ b/solution.py
@@ -27,7 +27,7 @@
                ids, rw, ns, es, tok, pick, rg0, rg1, rg2, own_codes, codes, c_send, p_buf, p_recv, x_rows, x_send, x_leg, x_back, x_acc,
                wg, wu, wd, send1, work, mid_r, hid, acc0, acc1, acc2, far0, far1, far2, near0, near1, near2,
                in_sem, w_sem, own_sem, send_sem, recv_sem, pair_send, pair_recv, a_send, a_recv, b_send, b_recv, c_ssem, c_rsem,
-               f_send, f_recv, n_send, n_recv, x_ssem, x_rsem, x_osem):
+               f_send, f_recv, n_send, n_recv, x_ssem, x_rsem, x_osem, l_send, l_recv, l_own, o_sem):
     f32, bf16 = jnp.float32, jnp.bfloat16
     tok_dev, d_model = tok_hbm.shape
     d_ff = wg_hbm.shape[1]
@@ -211,9 +211,9 @@
             idx[1 + dim] = index
             return ref.at[tuple(idx)]
 
-        remote = [to_ep(at(src, (pos[dim] + shift) % SIDE), at(dst, pos[dim]), x_ssem.at[leg, chunk % 2, v], x_rsem.at[leg, chunk, v], dim, shift)
+        remote = [to_ep(at(src, (pos[dim] + shift) % SIDE), at(dst, pos[dim]), x_ssem.at[leg, chunk, v], x_rsem.at[leg, chunk, v], dim, shift)
                   for v, shift in enumerate(SHIFTS)]
-        return remote + [pltpu.make_async_copy(at(src, pos[dim]), at(dst, pos[dim]), x_osem.at[leg, chunk % 2])]
+        return remote + [pltpu.make_async_copy(at(src, pos[dim]), at(dst, pos[dim]), x_osem.at[leg, chunk])]
 
     def x_launch(leg, chunk):
         for route_no in range(3):
@@ -230,17 +230,24 @@
                     c.wait()
 
     def x_gather(chunk):
-        for z in range(SIDE):
+        def pick_plane(z, carry):
             x_send[chunk % 2, z] = pick_slots(plane_codes(chunk, 0, z), own_codes, x_rows)
+            return carry
+
+        lax.fori_loop(0, SIDE, pick_plane, 0)
         x_launch(0, chunk)
 
     def x_combine(chunk):
         x_finish(5, chunk)
-        for z in range(SIDE):
+
+        def add_plane(z, carry):
             y = x_back[chunk, z].reshape(SIDE * SIDE * BLK, d_model - rest)
             want = plane_codes(chunk, 0, z)
             for n in range(2):
                 x_acc[n] += weigh_slots(want, own_codes, y, n)
+            return carry
+
+        lax.fori_loop(0, SIDE, add_plane, 0)
 
     x_acc[...] = jnp.zeros_like(x_acc)
     x_gather(0)
@@ -253,19 +260,25 @@
     for c in code_copies:
         c.wait()
 
+    def line(ref, slot, part, k, index):
+        idx = [slot, slice(None), slice(None), slice(None), slice(None), pl.ds(*cols[part])]
+        idx[1 + ROUTES[part][0]], idx[1 + ROUTES[part][1]] = k, index
+        return ref.at[tuple(idx)]
+
     def first_leg(chunk, part, k):
-        ring, dim = ROUTES[part][0], ROUTES[part][1]
-        c0, width = cols[part]
-
-        def line(ref, slot, index):
-            idx = [slot, slice(None), slice(None), slice(None), slice(None), pl.ds(c0, width)]
-            idx[1 + ring], idx[1 + dim] = k, index
-            return ref.at[tuple(idx)]
-
+        dim = ROUTES[part][1]
         for v, shift in enumerate(SHIFTS):
-            to_ep(line(send1, chunk % 2, (pos[dim] + shift) % SIDE), line(mid_d, chunk, pos[dim]),
+            to_ep(line(send1, chunk % 2, part, k, (pos[dim] + shift) % SIDE), line(mid_d, chunk, part, k, pos[dim]),
                   send_sem.at[0, chunk % 2, part, v], recv_sem.at[0, chunk, part, v], dim, shift).start()
-        pltpu.make_async_copy(line(send1, chunk % 2, pos[dim]), line(mid_d, chunk, pos[dim]), own_sem.at[0, chunk % 2, part]).start()
+        pltpu.make_async_copy(line(send1, chunk % 2, part, k, pos[dim]), line(mid_d, chunk, part, k, pos[dim]),
+                              own_sem.at[0, chunk % 2, part]).start()
+
+    def last_leg(chunk, part, v):
+        dim = ROUTES[part][1]
+        k = (pos[ROUTES[part][0]] + v) % SIDE
+        made = [to_ep(line(hop, chunk, part, k, (pos[dim] + shift) % SIDE), line(mid_r, chunk, part, k, pos[dim]),
+                      l_send.at[v, part, i], l_recv.at[v, part, i], dim, shift) for i, shift in enumerate(SHIFTS)]
+        return made + [pltpu.make_async_copy(line(hop, chunk, part, k, pos[dim]), line(mid_r, chunk, part, k, pos[dim]), l_own.at[v, part])]
 
     def gather(chunk):
         for v in (0, 3, 1, 2):
@@ -344,9 +357,12 @@
                 if stage < 4:
                     launch(stage, chunk)
                 else:
-                    for v in range(SIDE):
+                    def fold_source(v, carry):
                         for part in range(3):
                             fold(chunk, v, part)
+                        return carry
+
+                    lax.fori_loop(0, SIDE, fold_source, 0)
 
         @pl.when(t >= 5)
         def _():
@@ -354,7 +370,7 @@
 
         return carry
 
-    lax.fori_loop(0, n_chunks + 3, step, 0)
+    lax.fori_loop(0, n_chunks + 2, step, 0)
 
     def far_copies(part, n):
         dim = ROUTES[part][0]
@@ -362,61 +378,125 @@
         return [to_ep(accs[part].at[k, n, pl.ds(v * half, half)], fars[part].at[v, n], f_send.at[part, n, v], f_recv.at[part, n, v],
                       dim, (1, 3)[v]) for v in range(2)]
 
-    def near_copies(part, n):
+    first = (cols[0][1] // 128 + 1) // 2 * 128
+    pieces = ((0, first), (first, cols[0][1] - first))
+
+    def near_copies(part, n, piece):
         dim = ROUTES[part][0]
-        return [to_ep(accs[part].at[(pos[dim] + (1, 3)[v]) % SIDE, n], nears[part].at[v, n], n_send.at[part, n, v], n_recv.at[part, n, v],
-                      dim, (1, 3)[v]) for v in range(2)]
-
-    last = n_chunks - 1
-    finish(3, last)
-    for part in range(3):
-        fold(last, 2, part)
-        for c in far_copies(part, other):
-            c.start()
+        span = pl.ds(*pieces[piece])
+        return [to_ep(accs[part].at[(pos[dim] + (1, 3)[v]) % SIDE, n, :, span], nears[part].at[v, n, :, span],
+                      n_send.at[part, n, piece, v], n_recv.at[part, n, piece, v], dim, (1, 3)[v]) for v in range(2)]
+
+    last, prev = n_chunks - 1, n_chunks - 2
+
+    finish(2, last)
+    x_finish(3, last)
+
+    def start_source(i, carry):
+        for part in range(3):
+            for c in last_leg(last, part, (2 + 3 * i) % SIDE):
+                c.start()
+        return carry
+
+    lax.fori_loop(0, SIDE, start_source, 0)
+    x_launch(4, last)
+    finish(3, prev)
+    x_finish(4, prev)
+    x_launch(5, prev)
+
+    def fold_far(i, carry):
+        for part in range(3):
+            @pl.when(i == 1)
+            def _():
+                for c in last_leg(last, part, 2):
+                    c.wait()
+            fold(prev + i, 2, part)
+
+            @pl.when(i == 1)
+            def _():
+                for c in far_copies(part, other):
+                    c.start()
+        return carry
+
+    lax.fori_loop(0, 2, fold_far, 0)
     for part in range(3):
         for c in far_copies(part, node):
             c.start()
     x_finish(4, last)
     x_launch(5, last)
-    for v in (1, 3, 0):
-        for part in range(3):
-            fold(last, v, part)
+
+    def fold_rest(chunk, v):
+        for part in range(3):
+            @pl.when(chunk == last)
+            def _():
+                for c in last_leg(last, part, v):
+                    c.wait()
+            fold(chunk, v, part)
+
+    def fold_near(i, carry):
+        fold_rest(prev + i // 2, 1 + 2 * (i % 2))
+        return carry
+
+    lax.fori_loop(0, 4, fold_near, 0)
     for n in (other, node):
         for part in range(3):
             i = pos[ROUTES[part][0]]
             for v, c in enumerate(far_copies(part, n)):
                 c.wait()
                 accs[part][(i + (1, 3)[v]) % SIDE, n, v * half:(v + 1) * half] += fars[part][v, n]
-            for c in near_copies(part, n):
-                c.start()
-
-    for chunk in range(max(n_chunks - 2, 0), n_chunks):
-        x_combine(chunk)
-
-    def total(part, n):
-        for c in near_copies(part, n):
+        for piece in range(2):
+            for part in range(3):
+                for c in near_copies(part, n, piece):
+                    c.start()
+
+    def finish_own(i, carry):
+        fold_rest(prev + i, 0)
+        return carry
+
+    lax.fori_loop(0, 2, finish_own, 0)
+
+    def finish_x(i, carry):
+        x_combine(n_chunks - 3 + i)
+        return carry
+
+    lax.fori_loop(0, 3, finish_x, 0)
+
+    def total(part, n, piece):
+        for c in near_copies(part, n, piece):
             c.wait()
-        return (accs[part][pos[ROUTES[part][0]], n] + nears[part][0, n] + nears[part][1, n]).astype(bf16)
-
-    spans = [slice(c0, c0 + width) for c0, width in cols]
-    share = []
-    for part, at in enumerate(spans):
-        p_buf[other, :, at] = total(part, other)
-        share.append(to_pair(p_buf.at[other, :, pl.ds(*cols[part])], p_recv.at[:, pl.ds(*cols[part])], 4 + part))
-        share[-1].start()
+        at = slice(pieces[piece][0], pieces[piece][0] + pieces[piece][1])
+        return (accs[part][pos[ROUTES[part][0]], n, :, at] + nears[part][0, n, :, at] + nears[part][1, n, :, at]).astype(bf16)
+
+    def span_of(part, piece):
+        return slice(cols[part][0] + pieces[piece][0], cols[part][0] + pieces[piece][0] + pieces[piece][1])
+
+    def home(at, i):
+        c = pltpu.make_async_copy(tok.at[:, pl.ds(at.start, at.stop - at.start)], out_ref.at[:, pl.ds(at.start, at.stop - at.start)], o_sem.at[i])
+        c.start()
+        return c
+
+    for piece in range(2):
+        for part in range(3):
+            p_buf[other, :, span_of(part, piece)] = total(part, other, piece)
     p_buf[other, :, rest:] = x_acc[other].astype(bf16)
-    share.append(to_pair(p_buf.at[other, :, pl.ds(rest, d_model - rest)], p_recv.at[:, pl.ds(rest, d_model - rest)], 8))
-    share[-1].start()
-    for c in share:
+    share = to_pair(p_buf.at[other], p_recv, 4)
+    share.start()
+    x_sum = lax.dot_general(pick[node, :cap], x_acc[node].astype(bf16), TN, preferred_element_type=f32)
+    share.wait()
+    x_sum = x_sum + lax.dot_general(pick[other, :cap], p_recv[:, rest:], TN, preferred_element_type=f32)
+    tok[:, rest:] = x_sum.astype(bf16)
+    homes = [home(slice(rest, d_model), 0)]
+    for part in range(3):
+        at = slice(cols[part][0], cols[part][0] + cols[part][1])
+        tok[:, at] = lax.dot_general(pick[other, :cap], p_recv[:, at], TN, preferred_element_type=f32).astype(bf16)
+    for piece in range(2):
+        for part in range(3):
+            at = span_of(part, piece)
+            mine = lax.dot_general(pick[node, :cap], total(part, node, piece), TN, preferred_element_type=f32)
+            tok[:, at] = (tok[:, at].astype(f32) + mine).astype(bf16)
+            homes.append(home(at, 1 + piece * 3 + part))
+    for c in homes:
         c.wait()
-    x_sum = lax.dot_general(pick[other, :cap], p_recv[:, rest:], TN, preferred_element_type=f32)
-    x_sum = x_sum + lax.dot_general(pick[node, :cap], x_acc[node].astype(bf16), TN, preferred_element_type=f32)
-    out_ref[:, rest:] = x_sum.astype(bf16)
-    for at in spans:
-        out_ref[:, at] = lax.dot_general(pick[other, :cap], p_recv[:, at], TN, preferred_element_type=f32).astype(bf16)
-    for part, at in enumerate(spans):
-        mine = lax.dot_general(pick[node, :cap], total(part, node), TN, preferred_element_type=f32)
-        out_ref[:, at] = (out_ref[:, at].astype(f32) + mine).astype(bf16)
 
 
 def solution(mesh):
@@ -449,7 +529,7 @@
                        jax.ShapeDtypeStruct((n_chunks,) + cube, bf16),
                        jax.ShapeDtypeStruct((n_chunks,) + cube, bf16)),
             in_specs=[any_spec] * 8,
-            out_specs=(pl.BlockSpec(memory_space=pltpu.VMEM), any_spec, any_spec),
+            out_specs=(any_spec, any_spec, any_spec),
             scratch_shapes=[
                 pltpu.VMEM((top_k, tok_dev), i32), pltpu.VMEM((top_k, tok_dev), f32),
                 pltpu.VMEM((top_k, tok_dev), i32), pltpu.VMEM((top_k, tok_dev), i32),
@@ -468,8 +548,9 @@
                 *[pltpu.VMEM((2, 2, cap_node, width), f32) for _, width in part_columns(d_model)],
                 dma((5,)), dma((3,)), dma((4, 2, 3)), dma((4, 2, 3, 3)), dma((4, n_chunks, 3, 3)), dma((9,)), dma((9,)),
                 dma((3, 2, 2)), dma((3, 2, 2)), dma((3, 2, 2)), dma((3, 2, 2)), dma((3, 3)), dma((3, 3)),
-                dma((3, 2, 2)), dma((3, 2, 2)), dma((3, 2, 2)), dma((3, 2, 2)),
-                dma((6, 2, 3)), dma((6, n_chunks, 3)), dma((6, 2)),
+                dma((3, 2, 2)), dma((3, 2, 2)), dma((3, 2, 2, 2)), dma((3, 2, 2, 2)),
+                dma((6, n_chunks, 3)), dma((6, n_chunks, 3)), dma((6, n_chunks)),
+                dma((4, 3, 3)), dma((4, 3, 3)), dma((4, 3)), dma((7,)),
             ],
             compiler_params=pltpu.CompilerParams(collective_id=0, has_side_effects=True, vmem_limit_bytes=67_043_328),
         )(expert_ids.T, route_w.T, node_slot.T, exp_slot.T, tokens, w_gate[0], w_up[0], w_down[0])

time: 217 us -> 214 us (0.986)
    pallas_call x1, Pallas kernels: 213 us -> 211 us  [local_layer(): pl.pallas_call(functools.partial(moe_kernel, n_chunks), name='moe_layer',...]
where the time goes in v6:
time: 214 us; the launch traced here: 213 us
  Pallas kernels  211 us (99%)
  local copies, waits for them, and re-layouts  2.3 us (1%)
    pallas_call x1, Pallas kernels, local_layer(): pl.pallas_call(functools.partial(moe_kernel, n_chunks), name='moe_layer',...  211 us

profile of v6, /device:TPU:1, one launch (start us, length us, event | category | flops | bytes accessed | tf_op | source)
XLA Modules:
  0.0 213.2 jit_solution(10527052126256351061)
XLA Ops:
  0.0 210.9 %moe_layer.1 = (bf16[256,2048]{1,0:T(8,128)(2,1)}, bf16[5,4,4,4,8,2048]{5,4,3,2,1,0:T(8,128)(2,1)}, bf16[5,4,4,4,8,2048]{5,4,3,2,1,0:T(8,128)(2,1)}) custom-call(s32[8,256]{1,0:T(8,128)} %bitcast.10, f32[8,256]{1,0:T(8,128)} %bitcast.11, s32[8,256]{1,0:T(8,128)} %bitcast.12, s32[8,256]{1,0:T(8,128)} %bitcast.13, bf16[256,2048]{1,0:T(8,128)(2,1)} %tok_hbm.1, ...), custom_call_target="tpu_custom_call" | custom-call | tf_op jit(solution)/shard_map/moe_layer/pallas_call | solution.py:525
  210.9 2.3 %copy.10 = bf16[256,2048]{1,0:T(8,128)(2,1)} copy(bf16[256,2048]{1,0:T(8,128)(2,1)} %get-tuple-element.6) | data formatting | bytes 2097152

commit v7 on v6

--- a/solution.py
+++ b/solution.py
@@ -57,6 +57,10 @@
         return pltpu.make_async_remote_copy(src_ref=src, dst_ref=dst, send_sem=pair_send.at[i], recv_sem=pair_recv.at[i],
                                             device_id={"node": other}, device_id_type=MESH)
 
+    def drain(ref, *sems):
+        for sem in sems:
+            pltpu.make_async_copy(ref, ref, sem).wait()
+
     inputs = [pltpu.make_async_copy(s, d, in_sem.at[i]) for i, (s, d) in enumerate(
         ((ids_hbm, ids), (rw_hbm, rw), (ns_hbm, ns), (es_hbm, es), (tok_hbm, tok)))]
     weights = [pltpu.make_async_copy(s, d, w_sem.at[i]) for i, (s, d) in enumerate(((wg_hbm, wg), (wu_hbm, wu), (wd_hbm, wd)))]
@@ -99,12 +103,12 @@
     def ring_copies(part, n):
         dim, ring = ROUTES[part][0], rings[part]
         i = pos[dim]
-        first = [to_ep(ring.at[i, n], ring.at[i, n], a_send.at[part, n, v], a_recv.at[part, n, v], dim, (1, 3)[v]) for v in range(2)]
+        first = [to_ep(ring.at[i, n], ring.at[i, n], a_send.at[part, n], a_recv.at[part, n], dim, (1, 3)[v]) for v in range(2)]
         onward = []
         for v in range(2):
             k = (i + (3, 1)[v]) % SIDE
             span = pl.ds(v * half, half)
-            onward.append(to_ep(ring.at[k, n, span], ring.at[k, n, span], b_send.at[part, n, v], b_recv.at[part, n, v], dim, (1, 3)[v]))
+            onward.append(to_ep(ring.at[k, n, span], ring.at[k, n, span], b_send.at[part, n], b_recv.at[part, n], dim, (1, 3)[v]))
         return first, onward
 
     for part in range(3):
@@ -130,8 +134,8 @@
         for c in ring_copies(part, other)[0]:
             c.start()
     pair_codes.wait()
-    code_copies = [to_ep(own_codes, codes.at[dim, pos[dim]], c_ssem.at[dim, v], c_rsem.at[dim, v], dim, shift)
-                   for dim in range(3) for v, shift in enumerate(SHIFTS)]
+    code_copies = [to_ep(own_codes, codes.at[dim, pos[dim]], c_ssem.at[dim], c_rsem.at[dim], dim, shift)
+                   for dim in range(3) for shift in SHIFTS]
     for c in code_copies:
         c.start()
     for dim in range(3):
@@ -153,10 +157,10 @@
             for v, shift in enumerate(SHIFTS):
                 remote.append(to_ep(plane(src, src_chunk, dim, (pos[dim] + shift) % SIDE, part),
                                     plane(dst, chunk, dim, pos[dim], part),
-                                    send_sem.at[stage, chunk % 2, part, v], recv_sem.at[stage, chunk, part, v], dim, shift))
+                                    send_sem.at[stage, chunk % 2], recv_sem.at[stage, chunk], dim, shift))
             local.append(pltpu.make_async_copy(
                 plane(src, src_chunk, dim, pos[dim], part), plane(dst, chunk, dim, pos[dim], part),
-                own_sem.at[stage, chunk % 2, part]))
+                own_sem.at[stage, chunk % 2]))
         return remote, local
 
     def launch(stage, chunk):
@@ -166,12 +170,13 @@
         for c in local:
             c.start()
 
+    def all_of(ref, chunk, planes):
+        return ref.at[chunk, pl.ds(0, planes), :, :, :, pl.ds(0, rest)]
+
     def finish(stage, chunk):
-        remote, local = copies(stage, chunk)
-        for c in remote:
-            c.wait()
-        for c in local:
-            c.wait()
+        dst = stages[stage][1]
+        drain(all_of(dst, chunk, 3), send_sem.at[stage, chunk % 2], recv_sem.at[stage, chunk])
+        drain(all_of(dst, chunk, 1), own_sem.at[stage, chunk % 2])
 
     def plane_codes(chunk, dim, at):
         o0, o1 = [d for d in range(3) if d != dim]
@@ -211,8 +216,8 @@
             idx[1 + dim] = index
             return ref.at[tuple(idx)]
 
-        remote = [to_ep(at(src, (pos[dim] + shift) % SIDE), at(dst, pos[dim]), x_ssem.at[leg, chunk, v], x_rsem.at[leg, chunk, v], dim, shift)
-                  for v, shift in enumerate(SHIFTS)]
+        remote = [to_ep(at(src, (pos[dim] + shift) % SIDE), at(dst, pos[dim]), x_ssem.at[leg, chunk], x_rsem.at[leg, chunk], dim, shift)
+                  for shift in SHIFTS]
         return remote + [pltpu.make_async_copy(at(src, pos[dim]), at(dst, pos[dim]), x_osem.at[leg, chunk])]
 
     def x_launch(leg, chunk):
@@ -223,11 +228,8 @@
                     c.start()
 
     def x_finish(leg, chunk):
-        for route_no in range(3):
-            @pl.when(chunk % 3 == route_no)
-            def _():
-                for c in x_copies(leg, chunk, route_no):
-                    c.wait()
+        drain(x_leg.at[chunk, pl.ds(0, 3)], x_ssem.at[leg, chunk], x_rsem.at[leg, chunk])
+        drain(x_leg.at[chunk, 0], x_osem.at[leg, chunk])
 
     def x_gather(chunk):
         def pick_plane(z, carry):
@@ -253,12 +255,11 @@
     x_gather(0)
     for n in (node, other):
         for part in range(3):
-            first, onward = ring_copies(part, n)
-            for v in range(2):
-                first[v].wait()
-                onward[v].start()
-    for c in code_copies:
-        c.wait()
+            drain(rings[part].at[pl.ds(0, 2), n], a_send.at[part, n], a_recv.at[part, n])
+            for c in ring_copies(part, n)[1]:
+                c.start()
+    for dim in range(3):
+        drain(codes.at[dim, pl.ds(0, 3)], c_ssem.at[dim], c_rsem.at[dim])
 
     def line(ref, slot, part, k, index):
         idx = [slot, slice(None), slice(None), slice(None), slice(None), pl.ds(*cols[part])]
@@ -269,16 +270,20 @@
         dim = ROUTES[part][1]
         for v, shift in enumerate(SHIFTS):
             to_ep(line(send1, chunk % 2, part, k, (pos[dim] + shift) % SIDE), line(mid_d, chunk, part, k, pos[dim]),
-                  send_sem.at[0, chunk % 2, part, v], recv_sem.at[0, chunk, part, v], dim, shift).start()
+                  send_sem.at[0, chunk % 2], recv_sem.at[0, chunk], dim, shift).start()
         pltpu.make_async_copy(line(send1, chunk % 2, part, k, pos[dim]), line(mid_d, chunk, part, k, pos[dim]),
-                              own_sem.at[0, chunk % 2, part]).start()
+                              own_sem.at[0, chunk % 2]).start()
 
     def last_leg(chunk, part, v):
         dim = ROUTES[part][1]
         k = (pos[ROUTES[part][0]] + v) % SIDE
         made = [to_ep(line(hop, chunk, part, k, (pos[dim] + shift) % SIDE), line(mid_r, chunk, part, k, pos[dim]),
-                      l_send.at[v, part, i], l_recv.at[v, part, i], dim, shift) for i, shift in enumerate(SHIFTS)]
-        return made + [pltpu.make_async_copy(line(hop, chunk, part, k, pos[dim]), line(mid_r, chunk, part, k, pos[dim]), l_own.at[v, part])]
+                      l_send.at[v], l_recv.at[v], dim, shift) for shift in SHIFTS]
+        return made + [pltpu.make_async_copy(line(hop, chunk, part, k, pos[dim]), line(mid_r, chunk, part, k, pos[dim]), l_own.at[v])]
+
+    def last_finish(chunk, v):
+        drain(mid_r.at[chunk, 0, pl.ds(0, 3), :, :, pl.ds(0, rest)], l_send.at[v], l_recv.at[v])
+        drain(mid_r.at[chunk, 0, 0, :, :, pl.ds(0, rest)], l_own.at[v])
 
     def gather(chunk):
         for v in (0, 3, 1, 2):
@@ -287,8 +292,7 @@
                     @pl.when(chunk == 0)
                     def _():
                         for n in (node, other):
-                            for c in ring_copies(part, n)[1]:
-                                c.wait()
+                            drain(rings[part].at[0, n], b_send.at[part, n], b_recv.at[part, n])
                 dim = ROUTES[part][0]
                 k = (pos[dim] + v) % SIDE
                 c0, width = cols[part]
@@ -375,7 +379,7 @@
     def far_copies(part, n):
         dim = ROUTES[part][0]
         k = (pos[dim] + 2) % SIDE
-        return [to_ep(accs[part].at[k, n, pl.ds(v * half, half)], fars[part].at[v, n], f_send.at[part, n, v], f_recv.at[part, n, v],
+        return [to_ep(accs[part].at[k, n, pl.ds(v * half, half)], fars[part].at[v, n], f_send.at[part, n], f_recv.at[part, n],
                       dim, (1, 3)[v]) for v in range(2)]
 
     first = (cols[0][1] // 128 + 1) // 2 * 128
@@ -385,7 +389,7 @@
         dim = ROUTES[part][0]
         span = pl.ds(*pieces[piece])
         return [to_ep(accs[part].at[(pos[dim] + (1, 3)[v]) % SIDE, n, :, span], nears[part].at[v, n, :, span],
-                      n_send.at[part, n, piece, v], n_recv.at[part, n, piece, v], dim, (1, 3)[v]) for v in range(2)]
+                      n_send.at[part, n, piece], n_recv.at[part, n, piece], dim, (1, 3)[v]) for v in range(2)]
 
     last, prev = n_chunks - 1, n_chunks - 2
 
@@ -405,11 +409,11 @@
     x_launch(5, prev)
 
     def fold_far(i, carry):
-        for part in range(3):
-            @pl.when(i == 1)
-            def _():
-                for c in last_leg(last, part, 2):
-                    c.wait()
+        @pl.when(i == 1)
+        def _():
+            last_finish(last, 2)
+
+        for part in range(3):
             fold(prev + i, 2, part)
 
             @pl.when(i == 1)
@@ -426,11 +430,11 @@
     x_launch(5, last)
 
     def fold_rest(chunk, v):
-        for part in range(3):
-            @pl.when(chunk == last)
-            def _():
-                for c in last_leg(last, part, v):
-                    c.wait()
+        @pl.when(chunk == last)
+        def _():
+            last_finish(last, v)
+
+        for part in range(3):
             fold(chunk, v, part)
 
     def fold_near(i, carry):
@@ -441,8 +445,8 @@
     for n in (other, node):
         for part in range(3):
             i = pos[ROUTES[part][0]]
-            for v, c in enumerate(far_copies(part, n)):
-                c.wait()
+            drain(fars[part].at[:, n], f_send.at[part, n], f_recv.at[part, n])
+            for v in range(2):
                 accs[part][(i + (1, 3)[v]) % SIDE, n, v * half:(v + 1) * half] += fars[part][v, n]
         for piece in range(2):
             for part in range(3):
@@ -462,8 +466,7 @@
     lax.fori_loop(0, 3, finish_x, 0)
 
     def total(part, n, piece):
-        for c in near_copies(part, n, piece):
-            c.wait()
+        drain(nears[part].at[:, n, :, pl.ds(*pieces[piece])], n_send.at[part, n, piece], n_recv.at[part, n, piece])
         at = slice(pieces[piece][0], pieces[piece][0] + pieces[piece][1])
         return (accs[part][pos[ROUTES[part][0]], n, :, at] + nears[part][0, n, :, at] + nears[part][1, n, :, at]).astype(bf16)
 
@@ -546,11 +549,11 @@
                 *[pltpu.VMEM((SIDE, 2, cap_node, width), f32) for _, width in part_columns(d_model)],
                 *[pltpu.VMEM((2, 2, cap_node // 2, width), f32) for _, width in part_columns(d_model)],
                 *[pltpu.VMEM((2, 2, cap_node, width), f32) for _, width in part_columns(d_model)],
-                dma((5,)), dma((3,)), dma((4, 2, 3)), dma((4, 2, 3, 3)), dma((4, n_chunks, 3, 3)), dma((9,)), dma((9,)),
-                dma((3, 2, 2)), dma((3, 2, 2)), dma((3, 2, 2)), dma((3, 2, 2)), dma((3, 3)), dma((3, 3)),
-                dma((3, 2, 2)), dma((3, 2, 2)), dma((3, 2, 2, 2)), dma((3, 2, 2, 2)),
-                dma((6, n_chunks, 3)), dma((6, n_chunks, 3)), dma((6, n_chunks)),
-                dma((4, 3, 3)), dma((4, 3, 3)), dma((4, 3)), dma((7,)),
+                dma((5,)), dma((3,)), dma((4, 2)), dma((4, 2)), dma((4, n_chunks)), dma((9,)), dma((9,)),
+                dma((3, 2)), dma((3, 2)), dma((3, 2)), dma((3, 2)), dma((3,)), dma((3,)),
+                dma((3, 2)), dma((3, 2)), dma((3, 2, 2)), dma((3, 2, 2)),
+                dma((6, n_chunks)), dma((6, n_chunks)), dma((6, n_chunks)),
+                dma((4,)), dma((4,)), dma((4,)), dma((7,)),
             ],
             compiler_params=pltpu.CompilerParams(collective_id=0, has_side_effects=True, vmem_limit_bytes=67_043_328),
         )(expert_ids.T, route_w.T, node_slot.T, exp_slot.T, tokens, w_gate[0], w_up[0], w_down[0])

time: 214 us -> 210 us (0.981)
  Pallas kernels: 211 us -> 207 us
    pallas_call x1, Pallas kernels: 211 us -> 207 us  [local_layer(): pl.pallas_call(functools.partial(moe_kernel, n_chunks), name='moe_layer',...]
where the time goes in v7:
time: 210 us; the launch traced here: 209 us
  Pallas kernels  207 us (99%)
  local copies, waits for them, and re-layouts  2.3 us (1%)
    pallas_call x1, Pallas kernels, local_layer(): pl.pallas_call(functools.partial(moe_kernel, n_chunks), name='moe_layer',...  207 us

profile of v7, /device:TPU:1, one launch (start us, length us, event | category | flops | bytes accessed | tf_op | source)
XLA Modules:
  0.0 209.4 jit_solution(6214800924306667141)
XLA Ops:
  0.0 207.1 %moe_layer.1 = (bf16[256,2048]{1,0:T(8,128)(2,1)}, bf16[5,4,4,4,8,2048]{5,4,3,2,1,0:T(8,128)(2,1)}, bf16[5,4,4,4,8,2048]{5,4,3,2,1,0:T(8,128)(2,1)}) custom-call(s32[8,256]{1,0:T(8,128)} %bitcast.10, f32[8,256]{1,0:T(8,128)} %bitcast.11, s32[8,256]{1,0:T(8,128)} %bitcast.12, s32[8,256]{1,0:T(8,128)} %bitcast.13, bf16[256,2048]{1,0:T(8,128)(2,1)} %tok_hbm.1, ...), custom_call_target="tpu_custom_call" | custom-call | tf_op jit(solution)/shard_map/moe_layer/pallas_call | solution.py:528
  207.1 2.3 %copy.10 = bf16[256,2048]{1,0:T(8,128)(2,1)} copy(bf16[256,2048]{1,0:T(8,128)(2,1)} %get-tuple-element.6) | data formatting | bytes 2097152

commit v8 on v7

--- a/solution.py
+++ b/solution.py
@@ -116,8 +116,8 @@
             c.start()
     find_rows(other)
     p_buf[other] = jnp.dot(pick[other, :cap], tok[...], preferred_element_type=f32).astype(bf16)
-    pair = [to_pair(p_buf.at[other, :, pl.ds(*cols[part])], rings[part].at[pos[ROUTES[part][0]], node], part) for part in range(3)]
-    pair.append(to_pair(p_buf.at[other, :, pl.ds(rest, d_model - rest)], x_rows.at[node], 7))
+    pair = [to_pair(p_buf.at[other, :, pl.ds(*cols[part])], rings[part].at[pos[ROUTES[part][0]], node], 0) for part in range(3)]
+    pair.append(to_pair(p_buf.at[other, :, pl.ds(rest, d_model - rest)], x_rows.at[node], 0))
     for c in pair:
         c.start()
     c_send[...] = route(other)
@@ -128,8 +128,7 @@
         c.start()
     for acc in accs:
         acc[...] = jnp.zeros_like(acc)
-    for c in pair:
-        c.wait()
+    drain(p_buf.at[other], pair_send.at[0], pair_recv.at[0])
     for part in range(3):
         for c in ring_copies(part, other)[0]:
             c.start()
@@ -216,9 +215,9 @@
             idx[1 + dim] = index
             return ref.at[tuple(idx)]
 
-        remote = [to_ep(at(src, (pos[dim] + shift) % SIDE), at(dst, pos[dim]), x_ssem.at[leg, chunk], x_rsem.at[leg, chunk], dim, shift)
+        remote = [to_ep(at(src, (pos[dim] + shift) % SIDE), at(dst, pos[dim]), x_ssem.at[leg, chunk % 2], x_rsem.at[leg, chunk], dim, shift)
                   for shift in SHIFTS]
-        return remote + [pltpu.make_async_copy(at(src, pos[dim]), at(dst, pos[dim]), x_osem.at[leg, chunk])]
+        return remote + [pltpu.make_async_copy(at(src, pos[dim]), at(dst, pos[dim]), x_osem.at[leg, chunk % 2])]
 
     def x_launch(leg, chunk):
         for route_no in range(3):
@@ -228,8 +227,8 @@
                     c.start()
 
     def x_finish(leg, chunk):
-        drain(x_leg.at[chunk, pl.ds(0, 3)], x_ssem.at[leg, chunk], x_rsem.at[leg, chunk])
-        drain(x_leg.at[chunk, 0], x_osem.at[leg, chunk])
+        drain(x_leg.at[chunk, pl.ds(0, 3)], x_ssem.at[leg, chunk % 2], x_rsem.at[leg, chunk])
+        drain(x_leg.at[chunk, 0], x_osem.at[leg, chunk % 2])
 
     def x_gather(chunk):
         def pick_plane(z, carry):
@@ -426,6 +425,7 @@
     for part in range(3):
         for c in far_copies(part, node):
             c.start()
+    x_combine(n_chunks - 3)
     x_finish(4, last)
     x_launch(5, last)
 
@@ -460,10 +460,10 @@
     lax.fori_loop(0, 2, finish_own, 0)
 
     def finish_x(i, carry):
-        x_combine(n_chunks - 3 + i)
+        x_combine(prev + i)
         return carry
 
-    lax.fori_loop(0, 3, finish_x, 0)
+    lax.fori_loop(0, 2, finish_x, 0)
 
     def total(part, n, piece):
         drain(nears[part].at[:, n, :, pl.ds(*pieces[piece])], n_send.at[part, n, piece], n_recv.at[part, n, piece])
@@ -474,7 +474,7 @@
         return slice(cols[part][0] + pieces[piece][0], cols[part][0] + pieces[piece][0] + pieces[piece][1])
 
     def home(at, i):
-        c = pltpu.make_async_copy(tok.at[:, pl.ds(at.start, at.stop - at.start)], out_ref.at[:, pl.ds(at.start, at.stop - at.start)], o_sem.at[i])
+        c = pltpu.make_async_copy(tok.at[:, pl.ds(at.start, at.stop - at.start)], out_ref.at[:, pl.ds(at.start, at.stop - at.start)], o_sem.at[0])
         c.start()
         return c
 
@@ -498,8 +498,7 @@
             mine = lax.dot_general(pick[node, :cap], total(part, node, piece), TN, preferred_element_type=f32)
             tok[:, at] = (tok[:, at].astype(f32) + mine).astype(bf16)
             homes.append(home(at, 1 + piece * 3 + part))
-    for c in homes:
-        c.wait()
+    drain(tok, o_sem.at[0])
 
 
 def solution(mesh):
@@ -552,8 +551,8 @@
                 dma((5,)), dma((3,)), dma((4, 2)), dma((4, 2)), dma((4, n_chunks)), dma((9,)), dma((9,)),
                 dma((3, 2)), dma((3, 2)), dma((3, 2)), dma((3, 2)), dma((3,)), dma((3,)),
                 dma((3, 2)), dma((3, 2)), dma((3, 2, 2)), dma((3, 2, 2)),
-                dma((6, n_chunks)), dma((6, n_chunks)), dma((6, n_chunks)),
-                dma((4,)), dma((4,)), dma((4,)), dma((7,)),
+                dma((6, 2)), dma((6, n_chunks)), dma((6, 2)),
+                dma((4,)), dma((4,)), dma((4,)), dma((1,)),
             ],
             compiler_params=pltpu.CompilerParams(collective_id=0, has_side_effects=True, vmem_limit_bytes=67_043_328),
         )(expert_ids.T, route_w.T, node_slot.T, exp_slot.T, tokens, w_gate[0], w_up[0], w_down[0])

time: 210 us -> 209 us (level)
  no operation moved by 1% of the time
where the time goes in v8:
time: 209 us
  Pallas kernels  207 us (99%)
  local copies, waits for them, and re-layouts  2.3 us (1%)
    pallas_call x1, Pallas kernels, local_layer(): pl.pallas_call(functools.partial(moe_kernel, n_chunks), name='moe_layer',...  207 us

profile of v8, /device:TPU:1, one launch (start us, length us, event | category | flops | bytes accessed | tf_op | source)
XLA Modules:
  0.0 209.1 jit_solution(5885903930001963468)
XLA Ops:
  0.0 206.7 %moe_layer.1 = (bf16[256,2048]{1,0:T(8,128)(2,1)}, bf16[5,4,4,4,8,2048]{5,4,3,2,1,0:T(8,128)(2,1)}, bf16[5,4,4,4,8,2048]{5,4,3,2,1,0:T(8,128)(2,1)}) custom-call(s32[8,256]{1,0:T(8,128)} %bitcast.10, f32[8,256]{1,0:T(8,128)} %bitcast.11, s32[8,256]{1,0:T(8,128)} %bitcast.12, s32[8,256]{1,0:T(8,128)} %bitcast.13, bf16[256,2048]{1,0:T(8,128)(2,1)} %tok_hbm.1, ...), custom_call_target="tpu_custom_call" | custom-call | tf_op jit(solution)/shard_map/moe_layer/pallas_call | solution.py:527
  206.8 2.3 %copy.10 = bf16[256,2048]{1,0:T(8,128)(2,1)} copy(bf16[256,2048]{1,0:T(8,128)(2,1)} %get-tuple-element.6) | data formatting | bytes 2097152
